TPU v7x, 256 devices: a 2x2x32 block of a 4x8x32 slice. The times are simulated.
256 devices in a mesh: groups: 4 (over y, x), dp: 64 (over z, core).
Axes of the slice: x: 2, y: 2, z: 32, core: 2. Of those that a mesh axis runs over, the one named last changes fastest.
The devices are a block of a 4x8x32 slice.
Arguments:
- grads: bfloat16 [65536, 14336], P(('groups', 'dp')), parts along dimension 0, may hold values from -6 to 6
- inputs: bfloat16 [65536, 4096], P(('groups', 'dp')), parts along dimension 0, may hold values from -6 to 6
- lengths: int32 [512], P(('groups', 'dp')), parts along dimension 0, may hold values from 1 to 128
- left_rows: bfloat16 [3072, 14336], P(('groups', 'dp')), parts along dimension 0, may hold values from -0.046875 to 0.046875
- right_rows: bfloat16 [3072, 4096], P(('groups', 'dp')), parts along dimension 0, may hold values from -0.0014648438 to 0.0014648438
- owner_count: int32 [256], P(('groups', 'dp')), parts along dimension 0, may hold values from 0 to 12, as said below
Outputs:
- scores: float32 [512, 8], P(('groups', 'dp')), parts along dimension 0
There are 4 independent parts, one for each index of `groups`. A program takes and returns all parts, laid end to end along the dimension named above; each array names one. Nothing has to cross between parts.
Inputs may be any that keep to these rules, and one draw needn't show every extreme that they name: Index i of dp holds live factor rows in its first owner_count[i] slots, the rows offset_i to offset_i + owner_count[i] - 1 where offset_i is the sum of the counts of lower indices. The counts sum to 256, and some index holds 12.
All inputs are finite; a program needn't handle non-finite values.
Results may differ from a plain program's by a relative error of at most 0.0003.
Values may be sent and summed in bfloat16 or wider, within the bound.
No kernel may reach another device: no remote copies, remote signals or barrier semaphores. Data moves between devices by JAX's collectives and lax.ppermute only.
A program may use at most 192 MiB of HBM per device.

v0:
```python
import jax
import jax.numpy as jnp
from jax import lax
from jax.experimental import pallas as pl
from jax.experimental.pallas import tpu as pltpu
from jax.sharding import Mesh
from jax.sharding import PartitionSpec as P

RANK = 32
LEN = 128
LANES = 128
ROWS_DEV = 4
REACH = 2
CHAINS = 2
STRIP = 1024
PART = ("z", "core")
SPLIT = ("groups", "z", "core")
CONTRACT = (((1,), (1,)), ((), ()))
FLAT = (((1,), (0,)), ((), ()))


def two_way(chips, hops):
    right = [(2 * i + 1, 2 * ((i + hops) % chips) + 1) for i in range(chips)]
    left = [(2 * i, 2 * ((i - hops) % chips)) for i in range(chips)]
    return right + left


def swap(x):
    return lax.ppermute(x, "core", [(0, 1), (1, 0)])


def dot(a, b):
    return lax.dot_general(a, b, CONTRACT, preferred_element_type=jnp.float32)


def sums_of(grads, inputs, live, left, right):
    joined = dot(grads, left) * dot(inputs, right) * live[:, None]
    return jnp.sum(joined.reshape(-1, LEN, joined.shape[1]), axis=1)


def exact(sums, assign):
    return jnp.dot(sums, assign, precision=lax.Precision.HIGHEST)


def scored(blocks, grads, inputs, lens, assign):
    block = blocks[0][0].shape[0]
    flat = [(s, p, len(pieces), x) for s, pieces in enumerate(blocks) for p, x in enumerate(pieces)]
    tokens, ff = grads[0].shape
    width = ff + inputs[0].shape[1]
    rows, queries = assign.shape
    sides = len(grads)
    examples = sides * tokens // LEN
    wide = ff // STRIP
    steps = width // STRIP

    def body(lens_ref, *refs):
        (g0, g1, i0, i1, assign_ref), refs = refs[:5], refs[5:]
        parts, refs = refs[: len(flat)], refs[len(flat) :]
        out_ref, held, left, right, sems = refs
        k = pl.program_id(0)

        def move(i):
            s, p, n, x = flat[i]
            target = held.at[pl.ds(s * block, block), pl.ds(p * (width // n), width // n)]
            return pltpu.make_async_copy(parts[i], target, sems.at[i])

        @pl.when(k == 0)
        def _():
            for i in range(len(flat)):
                move(i).start()
            left[...] = jnp.zeros_like(left)
            right[...] = jnp.zeros_like(right)

            for i, (_, p, _, _) in enumerate(flat):
                if p == 0:
                    move(i).wait()

        @pl.when(k == width // CHAINS // STRIP)
        def _():
            for i, (_, p, _, _) in enumerate(flat):
                if p > 0:
                    move(i).wait()

        strip = held[:, pl.ds(k * STRIP, STRIP)]

        @pl.when(k < wide)
        def _():
            left[:tokens, :] += dot(g0[...], strip)
            left[tokens:, :] += dot(g1[...], strip)

        @pl.when(k >= wide)
        def _():
            right[:tokens, :] += dot(i0[...], strip)
            right[tokens:, :] += dot(i1[...], strip)

        @pl.when(k == steps - 1)
        def _():
            token = lax.broadcasted_iota(jnp.int32, (LEN, rows), 0)
            sums = []
            for e in range(examples):
                at = pl.ds(e * LEN, LEN)
                joined = left[at, :] * right[at, :]
                sums.append(jnp.sum(jnp.where(token < lens_ref[e], joined, 0.0), axis=0, keepdims=True))
            sums = jnp.concatenate(sums + [jnp.zeros_like(sums[0])] * (8 - examples), axis=0)
            out_ref[...] = exact(sums, assign_ref[...])

    wide_spec = pl.BlockSpec((tokens, STRIP), lambda k, _: (0, jnp.minimum(k, wide - 1)))
    slim_spec = pl.BlockSpec((tokens, STRIP), lambda k, _: (0, jnp.maximum(k - wide, 0)))
    whole = pl.BlockSpec((rows, queries), lambda k, _: (0, 0))
    anywhere = pl.BlockSpec(memory_space=pl.ANY)
    return pl.pallas_call(
        body,
        out_shape=jax.ShapeDtypeStruct((8, queries), jnp.float32),
        grid_spec=pltpu.PrefetchScalarGridSpec(
            num_scalar_prefetch=1,
            grid=(steps,),
            in_specs=[wide_spec, wide_spec, slim_spec, slim_spec, whole] + [anywhere] * len(flat),
            out_specs=pl.BlockSpec((8, queries), lambda k, _: (0, 0)),
            scratch_shapes=[
                pltpu.VMEM((rows, width), jnp.bfloat16),
                pltpu.VMEM((sides * tokens, rows), jnp.float32),
                pltpu.VMEM((sides * tokens, rows), jnp.float32),
                pltpu.SemaphoreType.DMA((len(flat),)),
            ],
        ),
        compiler_params=pltpu.CompilerParams(dimension_semantics=("arbitrary",)),
    )(lens, *grads, *inputs, assign, *[x for *_, x in flat])


def on_device(grads, inputs, lengths, left_rows, right_rows, owner_count):
    chips = lax.axis_size("z")
    z = lax.axis_index("z")
    core = lax.axis_index("core")
    devices = 2 * chips
    total = devices * ROWS_DEV
    queries = total // RANK
    block = total // chips
    cap = left_rows.shape[0]
    ff = left_rows.shape[1]
    width = ff + right_rows.shape[1]
    half = width // 2
    live = (jnp.arange(LEN, dtype=jnp.int32)[None, :] < lengths[:, None]).astype(jnp.float32).reshape(-1)

    own = jnp.concatenate([left_rows, right_rows], axis=1)
    packed = jnp.concatenate([own[:, :half], own[:, half:]], axis=0)
    small = jnp.concatenate([owner_count, lengths, jnp.zeros((LANES - 1 - lengths.shape[0],), jnp.int32)])
    notes = jnp.broadcast_to(small.astype(jnp.bfloat16)[None, :], (2 * cap, LANES))
    other = swap(jnp.concatenate([packed, notes], axis=1))
    notes = other[0, half:].astype(jnp.int32)
    other_count, lengths_s = notes[0], notes[1 : 1 + lengths.shape[0]]
    other = jnp.concatenate([other[:cap, :half], other[cap:, :half]], axis=1)
    first = core == 0
    raw = jnp.concatenate([jnp.where(first, own, other), jnp.where(first, other, own)], axis=0)

    n0 = jnp.where(first, owner_count[0], other_count)
    n1 = jnp.where(first, other_count, owner_count[0])
    slot = jnp.arange(2 * cap, dtype=jnp.int32)
    second = slot >= cap
    within = jnp.where(second, slot - cap, slot)
    valid = within < jnp.where(second, n1, n0)
    rank = jnp.where(valid, within + jnp.where(second, n0, 0), -1)
    lead = jnp.where(first, 0, n0 + n1 - 2 * block)
    edge_at = jnp.arange(2 * block, dtype=jnp.int32) + lead
    pick = (valid[None, :] & (rank[None, :] == edge_at[:, None])).astype(jnp.bfloat16)
    edge = lax.dot_general(pick, raw, FLAT, preferred_element_type=jnp.float32).astype(jnp.bfloat16)
    tip = jnp.where(first, edge[:block], edge[block:])
    me = 2 * z + core
    device_list = jnp.arange(devices, dtype=jnp.int32)
    one_hop = lax.ppermute(edge, PART, two_way(chips, 1))
    two_hops = lax.ppermute(tip, PART, two_way(chips, 2))
    counts = lax.psum(jnp.where(device_list == me, owner_count[0], 0), PART)
    one_hop, two_hops, counts = lax.optimization_barrier((one_hop, two_hops, counts))
    counts, grads_t, inputs_t = lax.optimization_barrier((counts, grads, inputs))
    grads_s, inputs_s = swap(grads_t), swap(inputs_t)
    pair = counts.reshape(chips, 2)
    held = jnp.sum(pair, axis=1)
    chip_list = jnp.arange(chips, dtype=jnp.int32)
    before = jnp.sum(jnp.where(chip_list[None, :] < chip_list[:, None], held[None, :], 0), axis=1)
    drift = before - block * chip_list
    low = jnp.min(drift)
    high = jnp.max(drift + held - 1)
    span = block * (2 * REACH + 1) - 1
    shift = jnp.floor_divide(block - 1 - low - high, 2)
    fits = high - low <= span

    place = jnp.arange(block, dtype=jnp.int32)
    side = jnp.where(first, 1, -1)

    def at(values, chip):
        return jnp.sum(jnp.where(chip_list == chip, values, 0))

    def chosen(rows, ranks, good, hops):
        source = jnp.remainder(z + side * hops, chips)
        spot = at(drift, source) + shift + block * side * hops + ranks
        sel = (good & (spot[None, :] == place[:, None])).astype(jnp.bfloat16)
        return lax.dot_general(sel, rows, FLAT, preferred_element_type=jnp.float32)

    def arrived(rows, hops):
        held_there = at(held, jnp.remainder(z + side * hops, chips))
        size = rows.shape[0]
        ranks = jnp.arange(size, dtype=jnp.int32) + jnp.where(first, 0, held_there - size)
        return chosen(rows, ranks, ((ranks >= 0) & (ranks < held_there))[None, :], hops)

    mine = chosen(raw, rank, (valid & ~first)[None, :], 0) + arrived(one_hop, 1) + arrived(two_hops, 2)
    mine = mine.astype(jnp.bfloat16)
    mine = mine + swap(mine)

    steps = chips // 2
    piece = width // CHAINS
    forth = two_way(chips, 1)
    near = lax.ppermute(mine, PART, forth)
    chains = [[near[:, i * piece : (i + 1) * piece]] for i in range(CHAINS)]
    for k in range(steps - 2):
        for i, chain in enumerate(chains):
            before_it = chains[i - 1]
            j = k if i > 0 else k - 1
            if j > 0:
                chain[k], before_it[j] = lax.optimization_barrier((chain[k], before_it[j]))
            chain.append(lax.ppermute(chain[k], PART, forth))
    last = lax.ppermute(jnp.concatenate([c[-1] for c in chains], axis=1), PART, forth)
    blocks = [[mine], [near]] + [[c[j] for c in chains] for j in range(1, steps - 1)] + [[last]]

    hop = jnp.repeat(jnp.arange(steps + 1, dtype=jnp.int32), block)
    counted = jnp.where(first, hop < steps, hop > 0)
    position = block * (z + jnp.where(first, hop, -hop)) + jnp.tile(place, steps + 1)
    query = jnp.remainder(position - shift, total) // RANK
    assign = (query[:, None] == jnp.arange(queries, dtype=jnp.int32)[None, :]) & counted[:, None]
    lens = jnp.concatenate([lengths, lengths_s])
    both = scored(blocks, (grads, grads_s), (inputs, inputs_s), lens, assign.astype(jnp.float32))
    mine_n = lengths.shape[0]
    fast = both[:mine_n] + swap(both[mine_n : 2 * mine_n])

    def general(fast, grads, inputs, live, raw):
        def step(k, carry):
            rows, out = carry
            source = jnp.remainder(z - k, chips)
            here = chip_list == source
            c0 = jnp.sum(jnp.where(here, pair[:, 0], 0))
            c1 = jnp.sum(jnp.where(here, pair[:, 1], 0))
            begin = jnp.sum(jnp.where(here, before, 0))
            valid = within < jnp.where(second, c1, c0)
            owner = (begin + within + jnp.where(second, c0, 0)) // RANK
            match = (owner[:, None] == jnp.arange(queries, dtype=jnp.int32)[None, :]) & valid[:, None]
            sums = sums_of(grads, inputs, live, rows[:, :ff], rows[:, ff:])
            out = out + exact(sums, match.astype(jnp.float32))
            return lax.ppermute(rows, "z", [(i, (i + 1) % chips) for i in range(chips)]), out

        return lax.fori_loop(0, chips, step, (raw, jnp.zeros_like(fast)))[1]

    return lax.cond(fits, lambda f, *_: f, general, fast, grads, inputs, live, raw)


def solution(mesh):
    groups, dp = mesh.devices.shape
    finer = Mesh(mesh.devices.reshape(groups, dp // 2, 2), SPLIT)
    return jax.shard_map(
        on_device,
        mesh=finer,
        in_specs=(
            P(SPLIT, None),
            P(SPLIT, None),
            P(SPLIT),
            P(SPLIT, None),
            P(SPLIT, None),
            P(SPLIT),
        ),
        out_specs=P(SPLIT, None),
        check_vma=False,
    )
```

profile of v0, /device:TPU:37, one launch (start us, length us, event | category | flops | bytes accessed | tf_op | source)
XLA Modules:
  0.0 209.4 jit_solution(4187183968181026368)
XLA Ops:
  0.0 1.1 constant_dynamic-update-slice_fusion.1
  1.8 0.7 convert.9
  2.4 0.9 constant_dynamic-update-slice_fusion
  3.6 20.5 %collective-permute-start.1 = (bf16[24,9344]{1,0:T(8,128)(2,1)S(1)}, bf16[24,9344]{1,0:T(8,128)(2,1)S(1)}, u32[]{:S(2)}, u32[]{:S(2)}) collective-permute-start(bf16[24,9344]{1,0:T(8,128)(2,1)S(1)} %maximum_maximum_fusion), channel_id=1, source_target_pairs={{0,1},{1,0},{2,3},{3,2},{4,5},{5,4},{6,7},{7,6},{8,9},{9,8},{10,11... | collective-permute-start | bytes 1345544 | tf_op jit(solution)/shard_map/ppermute | solution.py:29
  24.2 1.4 collective-permute-done.1
  26.1 1.1 pad_maximum_fusion
  27.2 1.5 convolution_convert_fusion
  29.1 31.6 %psum.7 = s32[64]{0:T(128)S(1)} all-reduce(s32[64]{0:T(128)S(1)} %compare_select_fusion.7), channel_id=1, replica_groups=mesh['groups'=4,'z'=32,'core'=2] {'z','core'}, use_global_device_ids=true, to_apply=%region_0.1 | all-reduce | flops 64 | bytes 512 | tf_op jit(solution)/shard_map/psum | solution.py:171
  61.1 0.8 fusion.37
  67.6 1.5 fusion.18
  69.0 1.4 convolution_add_fusion.2
  70.7 11.2 %collective-permute-start.6 = (bf16[8,18432]{1,0:T(8,128)(2,1)S(1)}, bf16[8,18432]{1,0:T(8,128)(2,1)S(1)}, u32[]{:S(2)}, u32[]{:S(2)}) collective-permute-start(bf16[8,18432]{1,0:T(8,128)(2,1)S(1)} %fusion.10), channel_id=1, source_target_pairs={{0,1},{1,0},{2,3},{3,2},{4,5},{5,4},{6,7},{7,6},{8,9},{9,8},{10,11... | collective-permute-start | bytes 884744 | tf_op jit(solution)/shard_map/ppermute | solution.py:29
  82.1 1.1 collective-permute-done.6
  83.4 6.8 %collective-permute-done.7.refs_6_ = bf16[8,18432]{1,0:T(8,128)(2,1)S(1)} collective-permute-done((bf16[8,18432]{1,0:T(8,128)(2,1)S(1)}, bf16[8,18432]{1,0:T(8,128)(2,1)S(1)}, u32[]{:S(2)}, u32[]{:S(2)}) %collective-permute-start.7) | collective-permute-done | bytes 294944 | tf_op jit(solution)/shard_map/ppermute | solution.py:211
  90.3 0.9 collective-permute-start.8
  91.2 4.3 %collective-permute-done.9.refs_7_ = bf16[8,9216]{1,0:T(8,128)(2,1)S(1)} collective-permute-done((bf16[8,9216]{1,0:T(8,128)(2,1)S(1)}, bf16[8,9216]{1,0:T(8,128)(2,1)S(1)}, u32[]{:S(2)}, u32[]{:S(2)}) %collective-permute-start.9) | collective-permute-done | bytes 147488 | tf_op jit(solution)/shard_map/ppermute | solution.py:219
  95.5 1.6 collective-permute-done.8.refs_8_
  97.0 3.6 %collective-permute-done.10.refs_9_ = bf16[8,9216]{1,0:T(8,128)(2,1)S(1)} collective-permute-done((bf16[8,9216]{1,0:T(8,128)(2,1)S(1)}, bf16[8,9216]{1,0:T(8,128)(2,1)S(1)}, u32[]{:S(2)}, u32[]{:S(2)}) %collective-permute-start.10) | collective-permute-done | bytes 147488 | tf_op jit(solution)/shard_map/ppermute | solution.py:219
  100.7 1.6 collective-permute-done.11.refs_10_
  102.3 3.6 %collective-permute-done.12.refs_11_ = bf16[8,9216]{1,0:T(8,128)(2,1)S(1)} collective-permute-done((bf16[8,9216]{1,0:T(8,128)(2,1)S(1)}, bf16[8,9216]{1,0:T(8,128)(2,1)S(1)}, u32[]{:S(2)}, u32[]{:S(2)}) %collective-permute-start.12) | collective-permute-done | bytes 147488 | tf_op jit(solution)/shard_map/ppermute | solution.py:219
  105.9 1.6 collective-permute-done.13.refs_12_
  107.5 3.6 %collective-permute-done.14.refs_13_ = bf16[8,9216]{1,0:T(8,128)(2,1)S(1)} collective-permute-done((bf16[8,9216]{1,0:T(8,128)(2,1)S(1)}, bf16[8,9216]{1,0:T(8,128)(2,1)S(1)}, u32[]{:S(2)}, u32[]{:S(2)}) %collective-permute-start.14) | collective-permute-done | bytes 147488 | tf_op jit(solution)/shard_map/ppermute | solution.py:219
  111.1 1.6 collective-permute-done.15.refs_14_
  112.7 3.6 %collective-permute-done.16.refs_15_ = bf16[8,9216]{1,0:T(8,128)(2,1)S(1)} collective-permute-done((bf16[8,9216]{1,0:T(8,128)(2,1)S(1)}, bf16[8,9216]{1,0:T(8,128)(2,1)S(1)}, u32[]{:S(2)}, u32[]{:S(2)}) %collective-permute-start.16) | collective-permute-done | bytes 147488 | tf_op jit(solution)/shard_map/ppermute | solution.py:219
  116.3 1.6 collective-permute-done.17.refs_16_
  117.9 3.6 %collective-permute-done.18.refs_17_ = bf16[8,9216]{1,0:T(8,128)(2,1)S(1)} collective-permute-done((bf16[8,9216]{1,0:T(8,128)(2,1)S(1)}, bf16[8,9216]{1,0:T(8,128)(2,1)S(1)}, u32[]{:S(2)}, u32[]{:S(2)}) %collective-permute-start.18) | collective-permute-done | bytes 147488 | tf_op jit(solution)/shard_map/ppermute | solution.py:219
  121.5 1.6 collective-permute-done.19.refs_18_
  123.1 3.6 %collective-permute-done.20.refs_19_ = bf16[8,9216]{1,0:T(8,128)(2,1)S(1)} collective-permute-done((bf16[8,9216]{1,0:T(8,128)(2,1)S(1)}, bf16[8,9216]{1,0:T(8,128)(2,1)S(1)}, u32[]{:S(2)}, u32[]{:S(2)}) %collective-permute-start.20) | collective-permute-done | bytes 147488 | tf_op jit(solution)/shard_map/ppermute | solution.py:219
  126.7 1.6 collective-permute-done.21.refs_20_
  128.3 3.6 %collective-permute-done.22.refs_21_ = bf16[8,9216]{1,0:T(8,128)(2,1)S(1)} collective-permute-done((bf16[8,9216]{1,0:T(8,128)(2,1)S(1)}, bf16[8,9216]{1,0:T(8,128)(2,1)S(1)}, u32[]{:S(2)}, u32[]{:S(2)}) %collective-permute-start.22) | collective-permute-done | bytes 147488 | tf_op jit(solution)/shard_map/ppermute | solution.py:219
  131.9 1.6 collective-permute-done.23.refs_22_
  133.5 3.6 %collective-permute-done.24.refs_23_ = bf16[8,9216]{1,0:T(8,128)(2,1)S(1)} collective-permute-done((bf16[8,9216]{1,0:T(8,128)(2,1)S(1)}, bf16[8,9216]{1,0:T(8,128)(2,1)S(1)}, u32[]{:S(2)}, u32[]{:S(2)}) %collective-permute-start.24) | collective-permute-done | bytes 147488 | tf_op jit(solution)/shard_map/ppermute | solution.py:219
  137.1 1.6 collective-permute-done.25.refs_24_
  138.7 3.7 %collective-permute-done.26.refs_25_ = bf16[8,9216]{1,0:T(8,128)(2,1)} collective-permute-done((bf16[8,9216]{1,0:T(8,128)(2,1)S(1)}, bf16[8,9216]{1,0:T(8,128)(2,1)}, u32[]{:S(2)}, u32[]{:S(2)}) %collective-permute-start.26) | collective-permute-done | bytes 147488 | tf_op jit(solution)/shard_map/ppermute | solution.py:219
  142.5 1.6 collective-permute-done.27.refs_26_
  144.1 3.8 %collective-permute-done.28.refs_27_ = bf16[8,9216]{1,0:T(8,128)(2,1)} collective-permute-done((bf16[8,9216]{1,0:T(8,128)(2,1)}, bf16[8,9216]{1,0:T(8,128)(2,1)}, u32[]{:S(2)}, u32[]{:S(2)}) %collective-permute-start.28) | collective-permute-done | bytes 147488 | tf_op jit(solution)/shard_map/ppermute | solution.py:219
  148.0 1.6 collective-permute-done.29.refs_28_
  149.6 3.9 %collective-permute-done.30.refs_29_ = bf16[8,9216]{1,0:T(8,128)(2,1)} collective-permute-done((bf16[8,9216]{1,0:T(8,128)(2,1)}, bf16[8,9216]{1,0:T(8,128)(2,1)}, u32[]{:S(2)}, u32[]{:S(2)}) %collective-permute-start.30) | collective-permute-done | bytes 147488 | tf_op jit(solution)/shard_map/ppermute | solution.py:219
  153.5 1.6 collective-permute-done.31.refs_30_
  155.2 3.8 %collective-permute-done.32.refs_31_ = bf16[8,9216]{1,0:T(8,128)(2,1)} collective-permute-done((bf16[8,9216]{1,0:T(8,128)(2,1)}, bf16[8,9216]{1,0:T(8,128)(2,1)}, u32[]{:S(2)}, u32[]{:S(2)}) %collective-permute-start.32) | collective-permute-done | bytes 147488 | tf_op jit(solution)/shard_map/ppermute | solution.py:219
  159.0 1.6 collective-permute-done.33.refs_32_
  161.2 16.5 %collective-permute-start.5 = (bf16[256,4096]{1,0:T(8,128)(2,1)S(1)}, bf16[256,4096]{1,0:T(8,128)(2,1)}, u32[]{:S(2)}, u32[]{:S(2)}) collective-permute-start(bf16[256,4096]{1,0:T(8,128)(2,1)S(1)} %copy-done), channel_id=1, source_target_pairs={{0,1},{1,0},{2,3},{3,2},{4,5},{5,4},{6,7},{7,6},{8,9},{9,8},{10,11... | collective-permute-start | bytes 6291464 | tf_op jit(solution)/shard_map/ppermute | solution.py:29
  179.3 0.7 fusion.12.refs_4_
  180.0 1.6 collective-permute-done.5.refs_3_
  181.6 3.2 %collective-permute-done.36.refs_35_ = bf16[8,18432]{1,0:T(8,128)(2,1)} collective-permute-done((bf16[8,18432]{1,0:T(8,128)(2,1)S(1)}, bf16[8,18432]{1,0:T(8,128)(2,1)}, u32[]{:S(2)}, u32[]{:S(2)}) %collective-permute-start.36) | collective-permute-done | bytes 294944 | tf_op jit(solution)/shard_map/ppermute | solution.py:220
  184.8 19.8 %shard_map.66 = f32[8,8]{1,0:T(8,128)S(1)} custom-call(s32[4]{0:T(128)} %pad_add_fusion.lens_ref, bf16[256,14336]{1,0:T(8,128)(2,1)} %refs_0_.1, bf16[256,14336]{1,0:T(8,128)(2,1)} %collective-permute-done.4.refs_1_, bf16[256,4096]{1,0:T(8,128)(2,1)S(1)} %copy-done, bf16[256,4096]{1,0:T(8,128)(2,1)} %collective-permute-done.5.refs_3_, ...), custom_call_target="tpu_custom_call" | custom-call | tf_op jit(solution)/shard_map/pallas_call | solution.py:111
  204.7 3.4 %collective-permute-start.37 = (f32[2,8]{1,0:T(2,128)S(1)}, f32[2,8]{1,0:T(2,128)S(1)}, u32[]{:S(2)}, u32[]{:S(2)}) collective-permute-start(f32[2,8]{1,0:T(2,128)S(1)} %slice.96), channel_id=1, source_target_pairs={{0,1},{1,0},{2,3},{3,2},{4,5},{5,4},{6,7},{7,6},{8,9},{9,8},{10,11... | collective-permute-start | bytes 200 | tf_op jit(solution)/shard_map/ppermute | solution.py:29
  208.1 0.8 collective-permute-done.37
  (130 shorter events, 5.1 us)
Async XLA Ops:
  3.6 22.0 %collective-permute-start.1 = (bf16[24,9344]{1,0:T(8,128)(2,1)S(1)}, bf16[24,9344]{1,0:T(8,128)(2,1)S(1)}, u32[]{:S(2)}, u32[]{:S(2)}) collective-permute-start(bf16[24,9344]{1,0:T(8,128)(2,1)S(1)} %maximum_maximum_fusion), channel_id=1, source_target_pairs={{0,1},{1,0},{2,3},{3,2},{4,5},{5,4},{6,7},{7,6},{8,9},{9,8},{10,11... | collective-permute-start | bytes 1345544 | tf_op jit(solution)/shard_map/ppermute | solution.py:29
  28.7 32.0 %collective-permute-start.2 = (bf16[16,18432]{1,0:T(8,128)(2,1)S(1)}, bf16[16,18432]{1,0:T(8,128)(2,1)S(1)}, u32[]{:S(2)}, u32[]{:S(2)}) collective-permute-start(bf16[16,18432]{1,0:T(8,128)(2,1)S(1)} %convolution_convert_fusion), channel_id=1, source_target_pairs={{1,3},{3,5},{5,7},{7,9},{9,11},{11,13},{13,15},{15,17},{17,19},{19... | collective-permute-start | bytes 1769480 | tf_op jit(solution)/shard_map/ppermute | solution.py:169
  28.9 31.8 %collective-permute-start.3 = (bf16[8,18432]{1,0:T(8,128)(2,1)S(1)}, bf16[8,18432]{1,0:T(8,128)(2,1)S(1)}, u32[]{:S(2)}, u32[]{:S(2)}) collective-permute-start(bf16[8,18432]{1,0:T(8,128)(2,1)S(1)} %slice_select_fusion), channel_id=1, source_target_pairs={{1,5},{3,7},{5,9},{7,11},{9,13},{11,15},{13,17},{15,19},{17,21},{1... | collective-permute-start | bytes 884744 | tf_op jit(solution)/shard_map/ppermute | solution.py:170
  69.0 80.5 %copy-start.24 = (s32[2]{0:T(128)S(1)}, s32[2]{0:T(128)}, u32[]{:S(2)}) copy-start(s32[2]{0:T(128)} %param.12) | copy-start | bytes 28
  69.0 92.2 %copy-start = (bf16[256,4096]{1,0:T(8,128)(2,1)S(1)}, bf16[256,4096]{1,0:T(8,128)(2,1)}, u32[]{:S(2)}) copy-start(bf16[256,4096]{1,0:T(8,128)(2,1)} %refs_2_.1) | copy-start | bytes 6291460
  70.7 12.4 %collective-permute-start.6 = (bf16[8,18432]{1,0:T(8,128)(2,1)S(1)}, bf16[8,18432]{1,0:T(8,128)(2,1)S(1)}, u32[]{:S(2)}, u32[]{:S(2)}) collective-permute-start(bf16[8,18432]{1,0:T(8,128)(2,1)S(1)} %fusion.10), channel_id=1, source_target_pairs={{0,1},{1,0},{2,3},{3,2},{4,5},{5,4},{6,7},{7,6},{8,9},{9,8},{10,11... | collective-permute-start | bytes 884744 | tf_op jit(solution)/shard_map/ppermute | solution.py:29
  81.9 102.9 %collective-permute-start.4 = (bf16[256,14336]{1,0:T(8,128)(2,1)}, bf16[256,14336]{1,0:T(8,128)(2,1)}, u32[]{:S(2)}, u32[]{:S(2)}) collective-permute-start(bf16[256,14336]{1,0:T(8,128)(2,1)} %refs_0_.1), channel_id=1, source_target_pairs={{0,1},{1,0},{2,3},{3,2},{4,5},{5,4},{6,7},{7,6},{8,9},{9,8},{10,11... | collective-permute-start | bytes 22020104 | tf_op jit(solution)/shard_map/ppermute | solution.py:29
  83.2 101.6 %copy-start.1 = (bf16[8,18432]{1,0:T(8,128)(2,1)}, bf16[8,18432]{1,0:T(8,128)(2,1)S(1)}, u32[]{:S(2)}) copy-start(bf16[8,18432]{1,0:T(8,128)(2,1)S(1)} %add.304.refs_5_) | copy-start | bytes 884740
  83.2 6.9 %collective-permute-start.7 = (bf16[8,18432]{1,0:T(8,128)(2,1)S(1)}, bf16[8,18432]{1,0:T(8,128)(2,1)S(1)}, u32[]{:S(2)}, u32[]{:S(2)}) collective-permute-start(bf16[8,18432]{1,0:T(8,128)(2,1)S(1)} %add.304.refs_5_), channel_id=1, source_target_pairs={{1,3},{3,5},{5,7},{7,9},{9,11},{11,13},{13,15},{15,17},{17,19},{19... | collective-permute-start | bytes 884744 | tf_op jit(solution)/shard_map/ppermute | solution.py:211
  90.1 94.7 %copy-start.2 = (bf16[8,18432]{1,0:T(8,128)(2,1)}, bf16[8,18432]{1,0:T(8,128)(2,1)S(1)}, u32[]{:S(2)}) copy-start(bf16[8,18432]{1,0:T(8,128)(2,1)S(1)} %collective-permute-done.7.refs_6_) | copy-start | bytes 884740
  90.1 5.3 %collective-permute-start.9 = (bf16[8,9216]{1,0:T(8,128)(2,1)S(1)}, bf16[8,9216]{1,0:T(8,128)(2,1)S(1)}, u32[]{:S(2)}, u32[]{:S(2)}) collective-permute-start(bf16[8,9216]{1,0:T(8,128)(2,1)S(1)} %get-tuple-element.630), channel_id=1, source_target_pairs={{1,3},{3,5},{5,7},{7,9},{9,11},{11,13},{13,15},{15,17},{17,19},{19... | collective-permute-start | bytes 442376 | tf_op jit(solution)/shard_map/ppermute | solution.py:219
  90.3 6.8 %collective-permute-start.8 = (bf16[8,9216]{1,0:T(8,128)(2,1)S(1)}, bf16[8,9216]{1,0:T(8,128)(2,1)S(1)}, u32[]{:S(2)}, u32[]{:S(2)}) collective-permute-start(bf16[8,9216]{1,0:T(8,128)(2,1)S(1)} %get-tuple-element.631), channel_id=1, source_target_pairs={{1,3},{3,5},{5,7},{7,9},{9,11},{11,13},{13,15},{15,17},{17,19},{19... | collective-permute-start | bytes 442376 | tf_op jit(solution)/shard_map/ppermute | solution.py:219
  95.5 89.3 %copy-start.6 = (bf16[8,9216]{1,0:T(8,128)(2,1)}, bf16[8,9216]{1,0:T(8,128)(2,1)S(1)}, u32[]{:S(2)}) copy-start(bf16[8,9216]{1,0:T(8,128)(2,1)S(1)} %collective-permute-done.9.refs_7_) | copy-start | bytes 442372
  95.5 5.2 %collective-permute-start.10 = (bf16[8,9216]{1,0:T(8,128)(2,1)S(1)}, bf16[8,9216]{1,0:T(8,128)(2,1)S(1)}, u32[]{:S(2)}, u32[]{:S(2)}) collective-permute-start(bf16[8,9216]{1,0:T(8,128)(2,1)S(1)} %collective-permute-done.9.refs_7_), channel_id=1, source_target_pairs={{1,3},{3,5},{5,7},{7,9},{9,11},{11,13},{13,15},{15,17},{17,19},{19... | collective-permute-start | bytes 442376 | tf_op jit(solution)/shard_map/ppermute | solution.py:219
  97.0 58.2 %copy-start.7 = (bf16[8,9216]{1,0:T(8,128)(2,1)}, bf16[8,9216]{1,0:T(8,128)(2,1)S(1)}, u32[]{:S(2)}) copy-start(bf16[8,9216]{1,0:T(8,128)(2,1)S(1)} %collective-permute-done.8.refs_8_) | copy-start | bytes 442372
  97.0 5.2 %collective-permute-start.11 = (bf16[8,9216]{1,0:T(8,128)(2,1)S(1)}, bf16[8,9216]{1,0:T(8,128)(2,1)S(1)}, u32[]{:S(2)}, u32[]{:S(2)}) collective-permute-start(bf16[8,9216]{1,0:T(8,128)(2,1)S(1)} %collective-permute-done.8.refs_8_), channel_id=1, source_target_pairs={{1,3},{3,5},{5,7},{7,9},{9,11},{11,13},{13,15},{15,17},{17,19},{19... | collective-permute-start | bytes 442376 | tf_op jit(solution)/shard_map/ppermute | solution.py:219
  100.7 58.3 %copy-start.8 = (bf16[8,9216]{1,0:T(8,128)(2,1)}, bf16[8,9216]{1,0:T(8,128)(2,1)S(1)}, u32[]{:S(2)}) copy-start(bf16[8,9216]{1,0:T(8,128)(2,1)S(1)} %collective-permute-done.10.refs_9_) | copy-start | bytes 442372
  100.7 5.2 %collective-permute-start.12 = (bf16[8,9216]{1,0:T(8,128)(2,1)S(1)}, bf16[8,9216]{1,0:T(8,128)(2,1)S(1)}, u32[]{:S(2)}, u32[]{:S(2)}) collective-permute-start(bf16[8,9216]{1,0:T(8,128)(2,1)S(1)} %collective-permute-done.10.refs_9_), channel_id=1, source_target_pairs={{1,3},{3,5},{5,7},{7,9},{9,11},{11,13},{13,15},{15,17},{17,19},{19... | collective-permute-start | bytes 442376 | tf_op jit(solution)/shard_map/ppermute | solution.py:219
  102.2 75.5 %copy-start.9 = (bf16[8,9216]{1,0:T(8,128)(2,1)}, bf16[8,9216]{1,0:T(8,128)(2,1)S(1)}, u32[]{:S(2)}) copy-start(bf16[8,9216]{1,0:T(8,128)(2,1)S(1)} %collective-permute-done.11.refs_10_) | copy-start | bytes 442372
  102.2 5.2 %collective-permute-start.13 = (bf16[8,9216]{1,0:T(8,128)(2,1)S(1)}, bf16[8,9216]{1,0:T(8,128)(2,1)S(1)}, u32[]{:S(2)}, u32[]{:S(2)}) collective-permute-start(bf16[8,9216]{1,0:T(8,128)(2,1)S(1)} %collective-permute-done.11.refs_10_), channel_id=1, source_target_pairs={{1,3},{3,5},{5,7},{7,9},{9,11},{11,13},{13,15},{15,17},{17,19},{19... | collective-permute-start | bytes 442376 | tf_op jit(solution)/shard_map/ppermute | solution.py:219
  105.9 71.8 %copy-start.10 = (bf16[8,9216]{1,0:T(8,128)(2,1)}, bf16[8,9216]{1,0:T(8,128)(2,1)S(1)}, u32[]{:S(2)}) copy-start(bf16[8,9216]{1,0:T(8,128)(2,1)S(1)} %collective-permute-done.12.refs_11_) | copy-start | bytes 442372
  105.9 5.2 %collective-permute-start.14 = (bf16[8,9216]{1,0:T(8,128)(2,1)S(1)}, bf16[8,9216]{1,0:T(8,128)(2,1)S(1)}, u32[]{:S(2)}, u32[]{:S(2)}) collective-permute-start(bf16[8,9216]{1,0:T(8,128)(2,1)S(1)} %collective-permute-done.12.refs_11_), channel_id=1, source_target_pairs={{1,3},{3,5},{5,7},{7,9},{9,11},{11,13},{13,15},{15,17},{17,19},{19... | collective-permute-start | bytes 442376 | tf_op jit(solution)/shard_map/ppermute | solution.py:219
  107.5 5.2 %collective-permute-start.15 = (bf16[8,9216]{1,0:T(8,128)(2,1)S(1)}, bf16[8,9216]{1,0:T(8,128)(2,1)S(1)}, u32[]{:S(2)}, u32[]{:S(2)}) collective-permute-start(bf16[8,9216]{1,0:T(8,128)(2,1)S(1)} %collective-permute-done.13.refs_12_), channel_id=1, source_target_pairs={{1,3},{3,5},{5,7},{7,9},{9,11},{11,13},{13,15},{15,17},{17,19},{19... | collective-permute-start | bytes 442376 | tf_op jit(solution)/shard_map/ppermute | solution.py:219
  111.1 5.2 %collective-permute-start.16 = (bf16[8,9216]{1,0:T(8,128)(2,1)S(1)}, bf16[8,9216]{1,0:T(8,128)(2,1)S(1)}, u32[]{:S(2)}, u32[]{:S(2)}) collective-permute-start(bf16[8,9216]{1,0:T(8,128)(2,1)S(1)} %collective-permute-done.14.refs_13_), channel_id=1, source_target_pairs={{1,3},{3,5},{5,7},{7,9},{9,11},{11,13},{13,15},{15,17},{17,19},{19... | collective-permute-start | bytes 442376 | tf_op jit(solution)/shard_map/ppermute | solution.py:219
  112.7 5.2 %collective-permute-start.17 = (bf16[8,9216]{1,0:T(8,128)(2,1)S(1)}, bf16[8,9216]{1,0:T(8,128)(2,1)S(1)}, u32[]{:S(2)}, u32[]{:S(2)}) collective-permute-start(bf16[8,9216]{1,0:T(8,128)(2,1)S(1)} %collective-permute-done.15.refs_14_), channel_id=1, source_target_pairs={{1,3},{3,5},{5,7},{7,9},{9,11},{11,13},{13,15},{15,17},{17,19},{19... | collective-permute-start | bytes 442376 | tf_op jit(solution)/shard_map/ppermute | solution.py:219
  116.3 5.2 %collective-permute-start.18 = (bf16[8,9216]{1,0:T(8,128)(2,1)S(1)}, bf16[8,9216]{1,0:T(8,128)(2,1)S(1)}, u32[]{:S(2)}, u32[]{:S(2)}) collective-permute-start(bf16[8,9216]{1,0:T(8,128)(2,1)S(1)} %collective-permute-done.16.refs_15_), channel_id=1, source_target_pairs={{1,3},{3,5},{5,7},{7,9},{9,11},{11,13},{13,15},{15,17},{17,19},{19... | collective-permute-start | bytes 442376 | tf_op jit(solution)/shard_map/ppermute | solution.py:219
  117.9 5.2 %collective-permute-start.19 = (bf16[8,9216]{1,0:T(8,128)(2,1)S(1)}, bf16[8,9216]{1,0:T(8,128)(2,1)S(1)}, u32[]{:S(2)}, u32[]{:S(2)}) collective-permute-start(bf16[8,9216]{1,0:T(8,128)(2,1)S(1)} %collective-permute-done.17.refs_16_), channel_id=1, source_target_pairs={{1,3},{3,5},{5,7},{7,9},{9,11},{11,13},{13,15},{15,17},{17,19},{19... | collective-permute-start | bytes 442376 | tf_op jit(solution)/shard_map/ppermute | solution.py:219
  121.5 5.2 %collective-permute-start.20 = (bf16[8,9216]{1,0:T(8,128)(2,1)S(1)}, bf16[8,9216]{1,0:T(8,128)(2,1)S(1)}, u32[]{:S(2)}, u32[]{:S(2)}) collective-permute-start(bf16[8,9216]{1,0:T(8,128)(2,1)S(1)} %collective-permute-done.18.refs_17_), channel_id=1, source_target_pairs={{1,3},{3,5},{5,7},{7,9},{9,11},{11,13},{13,15},{15,17},{17,19},{19... | collective-permute-start | bytes 442376 | tf_op jit(solution)/shard_map/ppermute | solution.py:219
  123.1 5.2 %collective-permute-start.21 = (bf16[8,9216]{1,0:T(8,128)(2,1)S(1)}, bf16[8,9216]{1,0:T(8,128)(2,1)S(1)}, u32[]{:S(2)}, u32[]{:S(2)}) collective-permute-start(bf16[8,9216]{1,0:T(8,128)(2,1)S(1)} %collective-permute-done.19.refs_18_), channel_id=1, source_target_pairs={{1,3},{3,5},{5,7},{7,9},{9,11},{11,13},{13,15},{15,17},{17,19},{19... | collective-permute-start | bytes 442376 | tf_op jit(solution)/shard_map/ppermute | solution.py:219
  126.7 5.2 %collective-permute-start.22 = (bf16[8,9216]{1,0:T(8,128)(2,1)S(1)}, bf16[8,9216]{1,0:T(8,128)(2,1)S(1)}, u32[]{:S(2)}, u32[]{:S(2)}) collective-permute-start(bf16[8,9216]{1,0:T(8,128)(2,1)S(1)} %collective-permute-done.20.refs_19_), channel_id=1, source_target_pairs={{1,3},{3,5},{5,7},{7,9},{9,11},{11,13},{13,15},{15,17},{17,19},{19... | collective-permute-start | bytes 442376 | tf_op jit(solution)/shard_map/ppermute | solution.py:219
  128.3 5.2 %collective-permute-start.23 = (bf16[8,9216]{1,0:T(8,128)(2,1)S(1)}, bf16[8,9216]{1,0:T(8,128)(2,1)S(1)}, u32[]{:S(2)}, u32[]{:S(2)}) collective-permute-start(bf16[8,9216]{1,0:T(8,128)(2,1)S(1)} %collective-permute-done.21.refs_20_), channel_id=1, source_target_pairs={{1,3},{3,5},{5,7},{7,9},{9,11},{11,13},{13,15},{15,17},{17,19},{19... | collective-permute-start | bytes 442376 | tf_op jit(solution)/shard_map/ppermute | solution.py:219
  131.9 5.2 %collective-permute-start.24 = (bf16[8,9216]{1,0:T(8,128)(2,1)S(1)}, bf16[8,9216]{1,0:T(8,128)(2,1)S(1)}, u32[]{:S(2)}, u32[]{:S(2)}) collective-permute-start(bf16[8,9216]{1,0:T(8,128)(2,1)S(1)} %collective-permute-done.22.refs_21_), channel_id=1, source_target_pairs={{1,3},{3,5},{5,7},{7,9},{9,11},{11,13},{13,15},{15,17},{17,19},{19... | collective-permute-start | bytes 442376 | tf_op jit(solution)/shard_map/ppermute | solution.py:219
  133.5 5.2 %collective-permute-start.25 = (bf16[8,9216]{1,0:T(8,128)(2,1)S(1)}, bf16[8,9216]{1,0:T(8,128)(2,1)S(1)}, u32[]{:S(2)}, u32[]{:S(2)}) collective-permute-start(bf16[8,9216]{1,0:T(8,128)(2,1)S(1)} %collective-permute-done.23.refs_22_), channel_id=1, source_target_pairs={{1,3},{3,5},{5,7},{7,9},{9,11},{11,13},{13,15},{15,17},{17,19},{19... | collective-permute-start | bytes 442376 | tf_op jit(solution)/shard_map/ppermute | solution.py:219
  137.1 5.3 %collective-permute-start.26 = (bf16[8,9216]{1,0:T(8,128)(2,1)S(1)}, bf16[8,9216]{1,0:T(8,128)(2,1)}, u32[]{:S(2)}, u32[]{:S(2)}) collective-permute-start(bf16[8,9216]{1,0:T(8,128)(2,1)S(1)} %collective-permute-done.24.refs_23_), channel_id=1, source_target_pairs={{1,3},{3,5},{5,7},{7,9},{9,11},{11,13},{13,15},{15,17},{17,19},{19... | collective-permute-start | bytes 442376 | tf_op jit(solution)/shard_map/ppermute | solution.py:219
  138.7 5.3 %collective-permute-start.27 = (bf16[8,9216]{1,0:T(8,128)(2,1)S(1)}, bf16[8,9216]{1,0:T(8,128)(2,1)}, u32[]{:S(2)}, u32[]{:S(2)}) collective-permute-start(bf16[8,9216]{1,0:T(8,128)(2,1)S(1)} %collective-permute-done.25.refs_24_), channel_id=1, source_target_pairs={{1,3},{3,5},{5,7},{7,9},{9,11},{11,13},{13,15},{15,17},{17,19},{19... | collective-permute-start | bytes 442376 | tf_op jit(solution)/shard_map/ppermute | solution.py:219
  142.4 5.5 %collective-permute-start.28 = (bf16[8,9216]{1,0:T(8,128)(2,1)}, bf16[8,9216]{1,0:T(8,128)(2,1)}, u32[]{:S(2)}, u32[]{:S(2)}) collective-permute-start(bf16[8,9216]{1,0:T(8,128)(2,1)} %collective-permute-done.26.refs_25_), channel_id=1, source_target_pairs={{1,3},{3,5},{5,7},{7,9},{9,11},{11,13},{13,15},{15,17},{17,19},{19... | collective-permute-start | bytes 442376 | tf_op jit(solution)/shard_map/ppermute | solution.py:219
  144.0 5.5 %collective-permute-start.29 = (bf16[8,9216]{1,0:T(8,128)(2,1)}, bf16[8,9216]{1,0:T(8,128)(2,1)}, u32[]{:S(2)}, u32[]{:S(2)}) collective-permute-start(bf16[8,9216]{1,0:T(8,128)(2,1)} %collective-permute-done.27.refs_26_), channel_id=1, source_target_pairs={{1,3},{3,5},{5,7},{7,9},{9,11},{11,13},{13,15},{15,17},{17,19},{19... | collective-permute-start | bytes 442376 | tf_op jit(solution)/shard_map/ppermute | solution.py:219
  148.0 5.5 %collective-permute-start.30 = (bf16[8,9216]{1,0:T(8,128)(2,1)}, bf16[8,9216]{1,0:T(8,128)(2,1)}, u32[]{:S(2)}, u32[]{:S(2)}) collective-permute-start(bf16[8,9216]{1,0:T(8,128)(2,1)} %collective-permute-done.28.refs_27_), channel_id=1, source_target_pairs={{1,3},{3,5},{5,7},{7,9},{9,11},{11,13},{13,15},{15,17},{17,19},{19... | collective-permute-start | bytes 442376 | tf_op jit(solution)/shard_map/ppermute | solution.py:219
  149.5 5.5 %collective-permute-start.31 = (bf16[8,9216]{1,0:T(8,128)(2,1)}, bf16[8,9216]{1,0:T(8,128)(2,1)}, u32[]{:S(2)}, u32[]{:S(2)}) collective-permute-start(bf16[8,9216]{1,0:T(8,128)(2,1)} %collective-permute-done.29.refs_28_), channel_id=1, source_target_pairs={{1,3},{3,5},{5,7},{7,9},{9,11},{11,13},{13,15},{15,17},{17,19},{19... | collective-permute-start | bytes 442376 | tf_op jit(solution)/shard_map/ppermute | solution.py:219
  153.5 5.5 %collective-permute-start.32 = (bf16[8,9216]{1,0:T(8,128)(2,1)}, bf16[8,9216]{1,0:T(8,128)(2,1)}, u32[]{:S(2)}, u32[]{:S(2)}) collective-permute-start(bf16[8,9216]{1,0:T(8,128)(2,1)} %collective-permute-done.30.refs_29_), channel_id=1, source_target_pairs={{1,3},{3,5},{5,7},{7,9},{9,11},{11,13},{13,15},{15,17},{17,19},{19... | collective-permute-start | bytes 442376 | tf_op jit(solution)/shard_map/ppermute | solution.py:219
  155.1 5.5 %collective-permute-start.33 = (bf16[8,9216]{1,0:T(8,128)(2,1)}, bf16[8,9216]{1,0:T(8,128)(2,1)}, u32[]{:S(2)}, u32[]{:S(2)}) collective-permute-start(bf16[8,9216]{1,0:T(8,128)(2,1)} %collective-permute-done.31.refs_30_), channel_id=1, source_target_pairs={{1,3},{3,5},{5,7},{7,9},{9,11},{11,13},{13,15},{15,17},{17,19},{19... | collective-permute-start | bytes 442376 | tf_op jit(solution)/shard_map/ppermute | solution.py:219
  159.0 18.7 %collective-permute-start.34 = (bf16[8,9216]{1,0:T(8,128)(2,1)}, bf16[8,9216]{1,0:T(8,128)(2,1)S(1)}, u32[]{:S(2)}, u32[]{:S(2)}) collective-permute-start(bf16[8,9216]{1,0:T(8,128)(2,1)} %collective-permute-done.32.refs_31_), channel_id=1, source_target_pairs={{1,3},{3,5},{5,7},{7,9},{9,11},{11,13},{13,15},{15,17},{17,19},{19... | collective-permute-start | bytes 442376 | tf_op jit(solution)/shard_map/ppermute | solution.py:219
  160.6 17.1 %collective-permute-start.35 = (bf16[8,9216]{1,0:T(8,128)(2,1)}, bf16[8,9216]{1,0:T(8,128)(2,1)S(1)}, u32[]{:S(2)}, u32[]{:S(2)}) collective-permute-start(bf16[8,9216]{1,0:T(8,128)(2,1)} %collective-permute-done.33.refs_32_), channel_id=1, source_target_pairs={{1,3},{3,5},{5,7},{7,9},{9,11},{11,13},{13,15},{15,17},{17,19},{19... | collective-permute-start | bytes 442376 | tf_op jit(solution)/shard_map/ppermute | solution.py:219
  161.2 20.4 %collective-permute-start.5 = (bf16[256,4096]{1,0:T(8,128)(2,1)S(1)}, bf16[256,4096]{1,0:T(8,128)(2,1)}, u32[]{:S(2)}, u32[]{:S(2)}) collective-permute-start(bf16[256,4096]{1,0:T(8,128)(2,1)S(1)} %copy-done), channel_id=1, source_target_pairs={{0,1},{1,0},{2,3},{3,2},{4,5},{5,4},{6,7},{7,6},{8,9},{9,8},{10,11... | collective-permute-start | bytes 6291464 | tf_op jit(solution)/shard_map/ppermute | solution.py:29
  177.7 7.1 %copy-start.4 = (bf16[8,9216]{1,0:T(8,128)(2,1)}, bf16[8,9216]{1,0:T(8,128)(2,1)S(1)}, u32[]{:S(2)}) copy-start(bf16[8,9216]{1,0:T(8,128)(2,1)S(1)} %collective-permute-done.35.refs_34_) | copy-start | bytes 442372
  177.7 7.1 %copy-start.3 = (bf16[8,9216]{1,0:T(8,128)(2,1)}, bf16[8,9216]{1,0:T(8,128)(2,1)S(1)}, u32[]{:S(2)}) copy-start(bf16[8,9216]{1,0:T(8,128)(2,1)S(1)} %collective-permute-done.34.refs_33_) | copy-start | bytes 442372
  177.8 7.0 %collective-permute-start.36 = (bf16[8,18432]{1,0:T(8,128)(2,1)S(1)}, bf16[8,18432]{1,0:T(8,128)(2,1)}, u32[]{:S(2)}, u32[]{:S(2)}) collective-permute-start(bf16[8,18432]{1,0:T(8,128)(2,1)S(1)} %pad_maximum_fusion.2), channel_id=1, source_target_pairs={{1,3},{3,5},{5,7},{7,9},{9,11},{11,13},{13,15},{15,17},{17,19},{19... | collective-permute-start | bytes 884744 | tf_op jit(solution)/shard_map/ppermute | solution.py:220
  204.7 4.2 %collective-permute-start.37 = (f32[2,8]{1,0:T(2,128)S(1)}, f32[2,8]{1,0:T(2,128)S(1)}, u32[]{:S(2)}, u32[]{:S(2)}) collective-permute-start(f32[2,8]{1,0:T(2,128)S(1)} %slice.96), channel_id=1, source_target_pairs={{0,1},{1,0},{2,3},{3,2},{4,5},{5,4},{6,7},{7,6},{8,9},{9,8},{10,11... | collective-permute-start | bytes 200 | tf_op jit(solution)/shard_map/ppermute | solution.py:29
  (16 other events, 45.8 us)
where the time goes:
time: 210 us; the launch traced here: 209 us
  waiting for transfers between devices  83.8 us (40%)
  starting transfers between devices  53.5 us (25%)
  blocking collectives  31.6 us (15%)
  Pallas kernels  19.8 us (9%)
  between operations  6.8 us (3%)
  other arithmetic  6.06 us (3%)
  matrix products  4.64 us (2%)
  local copies, waits for them, and re-layouts  3.17 us (2%)
    ppermute x28, waiting for transfers between devices, on_device(): chain.append(lax.ppermute(chain[k], PART, forth))  68.9 us
    ppermute x5, starting transfers between devices, swap(): return lax.ppermute(x, 'core', [(0, 1), (1, 0)])  51.8 us
    psum x1, blocking collectives, on_device(): counts = lax.psum(jnp.where(device_list == me, owner_count[0], 0), PART)  31.6 us
    pallas_call x1, Pallas kernels, scored(): pl.pallas_call(body, out_shape=jax.ShapeDtypeStruct((8, queries), jnp.flo...  19.8 us
    ppermute x1, waiting for transfers between devices, on_device(): near = lax.ppermute(mine, PART, forth)  6.76 us
    ppermute x5, waiting for transfers between devices, swap(): return lax.ppermute(x, 'core', [(0, 1), (1, 0)])  4.92 us
  transfers between devices with their start and end apart: 37, of which 32 were waited for; matrix products, arithmetic and copies ran while one was open for 1% of the time, Pallas kernels for 0%

commit v1 on v0

--- a/solution.py
+++ b/solution.py
@@ -12,7 +12,8 @@
 ROWS_DEV = 4
 REACH = 2
 CHAINS = 2
-STRIP = 1024
+PARTS = 3
+STRIP = 2048
 PART = ("z", "core")
 SPLIT = ("groups", "z", "core")
 CONTRACT = (((1,), (1,)), ((), ()))
@@ -42,19 +43,87 @@
     return jnp.dot(sums, assign, precision=lax.Precision.HIGHEST)
 
 
-def scored(blocks, grads, inputs, lens, assign):
+def log2(n):
+    assert n & (n - 1) == 0
+    return n.bit_length() - 1
+
+
+def routed_rows(raw, one_hop, two_hops, counts, seat, block):
+    chips = counts.shape[0] // 2
+    slots, width = raw.shape
+    cap = slots // 2
+    strip = width // PARTS
+
+    def body(counts_ref, seat_ref, raw_ref, one_ref, two_ref, out_ref, routed_ref, sel_ref, drift):
+        @pl.when(pl.program_id(0) == 0)
+        def _():
+            z, first = seat_ref[0], seat_ref[1] == 0
+            before, low, high = jnp.int32(0), jnp.int32(0), jnp.int32(0)
+            for y in range(chips):
+                drift[y] = before - block * y
+                low = jnp.minimum(low, drift[y])
+                before += counts_ref[2 * y] + counts_ref[2 * y + 1]
+                high = jnp.maximum(high, before - 1 - block * y)
+            shift = (block - 1 - low - high) >> 1
+            routed_ref[0] = shift
+            routed_ref[1] = (high - low <= block * (2 * REACH + 1) - 1).astype(jnp.int32)
+            side = jnp.where(first, 1, -1)
+            for h, size in enumerate((slots, 2 * block, block)):
+                source = (z + side * h) & (chips - 1)
+                c0, c1 = counts_ref[2 * source], counts_ref[2 * source + 1]
+                start = drift[source] + shift + block * side * h
+                slot = lax.broadcasted_iota(jnp.int32, (block, size), 1)
+                place = lax.broadcasted_iota(jnp.int32, (block, size), 0)
+                if h == 0:
+                    second = slot >= cap
+                    within = jnp.where(second, slot - cap, slot)
+                    rank = within + jnp.where(second, c0, 0)
+                    good = (within < jnp.where(second, c1, c0)) & (rank + jnp.where(first, 2 * slots, 0) < 2 * slots)
+                else:
+                    rank = slot + jnp.where(first, 0, c0 + c1 - size)
+                    good = (rank >= 0) & (rank < c0 + c1)
+                sel_ref[h, :, :size] = (good & (start + rank == place)).astype(jnp.float32)
+
+        taken = None
+        for h, ref in enumerate((raw_ref, one_ref, two_ref)):
+            sel = sel_ref[h, :, : ref.shape[0]].astype(jnp.bfloat16)
+            part = lax.dot_general(sel, ref[...], FLAT, preferred_element_type=jnp.float32)
+            taken = part if taken is None else taken + part
+        out_ref[...] = taken.astype(jnp.bfloat16)
+
+    log2(chips)
+
+    def spec(size):
+        return pl.BlockSpec((size, strip), lambda k, *_: (0, k))
+
+    return pl.pallas_call(
+        body,
+        out_shape=(jax.ShapeDtypeStruct((block, width), jnp.bfloat16), jax.ShapeDtypeStruct((2,), jnp.int32)),
+        grid_spec=pltpu.PrefetchScalarGridSpec(
+            num_scalar_prefetch=2,
+            grid=(PARTS,),
+            in_specs=[spec(slots), spec(2 * block), spec(block)],
+            out_specs=(spec(block), pl.BlockSpec(memory_space=pltpu.SMEM)),
+            scratch_shapes=[pltpu.VMEM((3, block, LANES), jnp.float32), pltpu.SMEM((chips,), jnp.int32)],
+        ),
+        compiler_params=pltpu.CompilerParams(dimension_semantics=("arbitrary",)),
+    )(counts, seat, raw, one_hop, two_hops)
+
+
+def scored(blocks, grads, inputs, lens, seat, routed, chips, total):
     block = blocks[0][0].shape[0]
     flat = [(s, p, len(pieces), x) for s, pieces in enumerate(blocks) for p, x in enumerate(pieces)]
     tokens, ff = grads[0].shape
     width = ff + inputs[0].shape[1]
-    rows, queries = assign.shape
+    rows = len(blocks) * block
+    queries = total // RANK
     sides = len(grads)
     examples = sides * tokens // LEN
     wide = ff // STRIP
     steps = width // STRIP
 
-    def body(lens_ref, *refs):
-        (g0, g1, i0, i1, assign_ref), refs = refs[:5], refs[5:]
+    def body(lens_ref, seat_ref, routed_ref, *refs):
+        (g0, g1, i0, i1), refs = refs[:4], refs[4:]
         parts, refs = refs[: len(flat)], refs[len(flat) :]
         out_ref, held, left, right, sems = refs
         k = pl.program_id(0)
@@ -102,20 +171,27 @@
                 joined = left[at, :] * right[at, :]
                 sums.append(jnp.sum(jnp.where(token < lens_ref[e], joined, 0.0), axis=0, keepdims=True))
             sums = jnp.concatenate(sums + [jnp.zeros_like(sums[0])] * (8 - examples), axis=0)
-            out_ref[...] = exact(sums, assign_ref[...])
-
-    wide_spec = pl.BlockSpec((tokens, STRIP), lambda k, _: (0, jnp.minimum(k, wide - 1)))
-    slim_spec = pl.BlockSpec((tokens, STRIP), lambda k, _: (0, jnp.maximum(k - wide, 0)))
-    whole = pl.BlockSpec((rows, queries), lambda k, _: (0, 0))
+            row = lax.broadcasted_iota(jnp.int32, (rows, queries), 0)
+            hop = row >> log2(block)
+            first = seat_ref[1] == 0
+            chip = seat_ref[0] + jnp.where(first, hop, -hop)
+            position = block * chip + (row & (block - 1)) - routed_ref[0]
+            query = (position & (total - 1)) >> log2(RANK)
+            counted = (hop >= jnp.where(first, 0, 1)) & (hop < jnp.where(first, chips // 2, chips))
+            match = (query == lax.broadcasted_iota(jnp.int32, (rows, queries), 1)) & counted
+            out_ref[...] = exact(sums, match.astype(jnp.float32))
+
+    wide_spec = pl.BlockSpec((tokens, STRIP), lambda k, *_: (0, jnp.minimum(k, wide - 1)))
+    slim_spec = pl.BlockSpec((tokens, STRIP), lambda k, *_: (0, jnp.maximum(k - wide, 0)))
     anywhere = pl.BlockSpec(memory_space=pl.ANY)
     return pl.pallas_call(
         body,
         out_shape=jax.ShapeDtypeStruct((8, queries), jnp.float32),
         grid_spec=pltpu.PrefetchScalarGridSpec(
-            num_scalar_prefetch=1,
+            num_scalar_prefetch=3,
             grid=(steps,),
-            in_specs=[wide_spec, wide_spec, slim_spec, slim_spec, whole] + [anywhere] * len(flat),
-            out_specs=pl.BlockSpec((8, queries), lambda k, _: (0, 0)),
+            in_specs=[wide_spec, wide_spec, slim_spec, slim_spec] + [anywhere] * len(flat),
+            out_specs=pl.BlockSpec((8, queries), lambda k, *_: (0, 0)),
             scratch_shapes=[
                 pltpu.VMEM((rows, width), jnp.bfloat16),
                 pltpu.VMEM((sides * tokens, rows), jnp.float32),
@@ -124,7 +200,7 @@
             ],
         ),
         compiler_params=pltpu.CompilerParams(dimension_semantics=("arbitrary",)),
-    )(lens, *grads, *inputs, assign, *[x for *_, x in flat])
+    )(lens, seat, routed, *grads, *inputs, *[x for *_, x in flat])
 
 
 def on_device(grads, inputs, lengths, left_rows, right_rows, owner_count):
@@ -164,45 +240,16 @@
     pick = (valid[None, :] & (rank[None, :] == edge_at[:, None])).astype(jnp.bfloat16)
     edge = lax.dot_general(pick, raw, FLAT, preferred_element_type=jnp.float32).astype(jnp.bfloat16)
     tip = jnp.where(first, edge[:block], edge[block:])
-    me = 2 * z + core
     device_list = jnp.arange(devices, dtype=jnp.int32)
     one_hop = lax.ppermute(edge, PART, two_way(chips, 1))
     two_hops = lax.ppermute(tip, PART, two_way(chips, 2))
-    counts = lax.psum(jnp.where(device_list == me, owner_count[0], 0), PART)
+    held_here = jnp.where(device_list == 2 * z, n0, jnp.where(device_list == 2 * z + 1, n1, 0))
+    counts = lax.psum(held_here, "z")
     one_hop, two_hops, counts = lax.optimization_barrier((one_hop, two_hops, counts))
     counts, grads_t, inputs_t = lax.optimization_barrier((counts, grads, inputs))
     grads_s, inputs_s = swap(grads_t), swap(inputs_t)
-    pair = counts.reshape(chips, 2)
-    held = jnp.sum(pair, axis=1)
-    chip_list = jnp.arange(chips, dtype=jnp.int32)
-    before = jnp.sum(jnp.where(chip_list[None, :] < chip_list[:, None], held[None, :], 0), axis=1)
-    drift = before - block * chip_list
-    low = jnp.min(drift)
-    high = jnp.max(drift + held - 1)
-    span = block * (2 * REACH + 1) - 1
-    shift = jnp.floor_divide(block - 1 - low - high, 2)
-    fits = high - low <= span
-
-    place = jnp.arange(block, dtype=jnp.int32)
-    side = jnp.where(first, 1, -1)
-
-    def at(values, chip):
-        return jnp.sum(jnp.where(chip_list == chip, values, 0))
-
-    def chosen(rows, ranks, good, hops):
-        source = jnp.remainder(z + side * hops, chips)
-        spot = at(drift, source) + shift + block * side * hops + ranks
-        sel = (good & (spot[None, :] == place[:, None])).astype(jnp.bfloat16)
-        return lax.dot_general(sel, rows, FLAT, preferred_element_type=jnp.float32)
-
-    def arrived(rows, hops):
-        held_there = at(held, jnp.remainder(z + side * hops, chips))
-        size = rows.shape[0]
-        ranks = jnp.arange(size, dtype=jnp.int32) + jnp.where(first, 0, held_there - size)
-        return chosen(rows, ranks, ((ranks >= 0) & (ranks < held_there))[None, :], hops)
-
-    mine = chosen(raw, rank, (valid & ~first)[None, :], 0) + arrived(one_hop, 1) + arrived(two_hops, 2)
-    mine = mine.astype(jnp.bfloat16)
+    seat = jnp.stack([z, core]).astype(jnp.int32)
+    mine, routed = routed_rows(raw, one_hop, two_hops, counts, seat, block)
     mine = mine + swap(mine)
 
     steps = chips // 2
@@ -220,17 +267,17 @@
     last = lax.ppermute(jnp.concatenate([c[-1] for c in chains], axis=1), PART, forth)
     blocks = [[mine], [near]] + [[c[j] for c in chains] for j in range(1, steps - 1)] + [[last]]
 
-    hop = jnp.repeat(jnp.arange(steps + 1, dtype=jnp.int32), block)
-    counted = jnp.where(first, hop < steps, hop > 0)
-    position = block * (z + jnp.where(first, hop, -hop)) + jnp.tile(place, steps + 1)
-    query = jnp.remainder(position - shift, total) // RANK
-    assign = (query[:, None] == jnp.arange(queries, dtype=jnp.int32)[None, :]) & counted[:, None]
     lens = jnp.concatenate([lengths, lengths_s])
-    both = scored(blocks, (grads, grads_s), (inputs, inputs_s), lens, assign.astype(jnp.float32))
+    both = scored(blocks, (grads, grads_s), (inputs, inputs_s), lens, seat, routed, chips, total)
     mine_n = lengths.shape[0]
     fast = both[:mine_n] + swap(both[mine_n : 2 * mine_n])
 
     def general(fast, grads, inputs, live, raw):
+        pair = counts.reshape(chips, 2)
+        held = jnp.sum(pair, axis=1)
+        chip_list = jnp.arange(chips, dtype=jnp.int32)
+        before = jnp.cumsum(held) - held
+
         def step(k, carry):
             rows, out = carry
             source = jnp.remainder(z - k, chips)
@@ -247,7 +294,7 @@
 
         return lax.fori_loop(0, chips, step, (raw, jnp.zeros_like(fast)))[1]
 
-    return lax.cond(fits, lambda f, *_: f, general, fast, grads, inputs, live, raw)
+    return lax.cond(routed[1] == 1, lambda f, *_: f, general, fast, grads, inputs, live, raw)
 
 
 def solution(mesh):

time: 210 us -> 207 us (0.986)
  between operations: 6.8 us -> 1.91 us
  local copies, waits for them, and re-layouts: 3.17 us -> 6.28 us
  matrix products: 4.64 us -> 1.53 us
  waiting for transfers between devices: 83.8 us -> 86.9 us
    ppermute x5, waiting for transfers between devices: 4.92 us -> 10.1 us  [swap(): return lax.ppermute(x, 'core', [(0, 1), (1, 0)])]
    pallas_call x1, Pallas kernels: 19.8 us -> 15.5 us  [scored(): pl.pallas_call(body, out_shape=jax.ShapeDtypeStruct((8, queries), jnp.flo...]
    pallas_call x0 -> x1, Pallas kernels: none -> 4.13 us  [routed_rows(): pl.pallas_call(body, out_shape=(jax.ShapeDtypeStruct((block, width), jnp....]
    dot_general x3 -> x0, matrix products: 3.11 us -> none  [chosen(): return lax.dot_general(sel, rows, FLAT, preferred_element_type=jnp.float32)]
  transfers between devices with their start and end apart: 37 -> 37, of which waited for: 32 -> 32; matrix products, arithmetic and copies ran while one was open for 1% -> 2% of each run, Pallas kernels for 0% -> 2%
where the time goes in v1:
time: 207 us
  waiting for transfers between devices  86.9 us (42%)
  starting transfers between devices  54.9 us (27%)
  blocking collectives  30.8 us (15%)
  Pallas kernels  19.7 us (10%)
  local copies, waits for them, and re-layouts  6.28 us (3%)
  other arithmetic  4.63 us (2%)
    ppermute x28, waiting for transfers between devices, on_device(): chain.append(lax.ppermute(chain[k], PART, forth))  68.2 us
    ppermute x5, starting transfers between devices, swap(): return lax.ppermute(x, 'core', [(0, 1), (1, 0)])  53 us
    psum x1, blocking collectives, on_device(): counts = lax.psum(held_here, 'z')  30.8 us
    pallas_call x1, Pallas kernels, scored(): pl.pallas_call(body, out_shape=jax.ShapeDtypeStruct((8, queries), jnp.flo...  15.5 us
    ppermute x5, waiting for transfers between devices, swap(): return lax.ppermute(x, 'core', [(0, 1), (1, 0)])  10.1 us
    ppermute x1, waiting for transfers between devices, on_device(): near = lax.ppermute(mine, PART, forth)  6.76 us
  transfers between devices with their start and end apart: 37, of which 32 were waited for; matrix products, arithmetic and copies ran while one was open for 2% of the time, Pallas kernels for 2%

profile of v1, /device:TPU:37, one launch (start us, length us, event | category | flops | bytes accessed | tf_op | source)
XLA Modules:
  0.0 206.6 jit_solution(10869498747665728934)
XLA Ops:
  0.0 1.1 constant_dynamic-update-slice_fusion.1
  1.8 0.7 convert.10
  2.4 0.9 constant_dynamic-update-slice_fusion
  3.6 20.5 %collective-permute-start.1 = (bf16[24,9344]{1,0:T(8,128)(2,1)S(1)}, bf16[24,9344]{1,0:T(8,128)(2,1)S(1)}, u32[]{:S(2)}, u32[]{:S(2)}) collective-permute-start(bf16[24,9344]{1,0:T(8,128)(2,1)S(1)} %maximum_maximum_fusion), channel_id=1, source_target_pairs={{0,1},{1,0},{2,3},{3,2},{4,5},{5,4},{6,7},{7,6},{8,9},{9,8},{10,11... | collective-permute-start | bytes 1345544 | tf_op jit(solution)/shard_map/ppermute | solution.py:30
  24.2 1.4 collective-permute-done.1
  26.0 1.1 pad_maximum_fusion.raw_ref
  27.2 1.5 convolution_convert_fusion
  29.1 30.8 %psum.7.counts_ref = s32[64]{0:T(128)S(1)} all-reduce(s32[64]{0:T(128)S(1)} %compare_select_fusion.4), channel_id=1, replica_groups=mesh['groups'=4,'z'=32,'core'=2] {'z'}, use_global_device_ids=true, to_apply=%region_0.1 | all-reduce | flops 64 | bytes 512 | tf_op jit(solution)/shard_map/psum | solution.py:247
  59.9 12.1 %collective-permute-start.4 = (bf16[256,14336]{1,0:T(8,128)(2,1)}, bf16[256,14336]{1,0:T(8,128)(2,1)}, u32[]{:S(2)}, u32[]{:S(2)}) collective-permute-start(bf16[256,14336]{1,0:T(8,128)(2,1)} %refs_0_.1), channel_id=1, source_target_pairs={{0,1},{1,0},{2,3},{3,2},{4,5},{5,4},{6,7},{7,6},{8,9},{9,8},{10,11... | collective-permute-start | bytes 22020104 | tf_op jit(solution)/shard_map/ppermute | solution.py:30
  72.6 4.1 %shard_map.66 = (bf16[8,18432]{1,0:T(8,128)(2,1)}, s32[2]{0:T(128)}) custom-call(s32[64]{0:T(128)S(1)} %psum.7.counts_ref, s32[2]{0:T(128)} %pad_add_fusion.seat_ref, bf16[24,18432]{1,0:T(8,128)(2,1)} %pad_maximum_fusion.raw_ref, bf16[16,18432]{1,0:T(8,128)(2,1)} %collective-permute-done.2.one_ref, bf16[8,18432]{1,0:T(8,128)(2,1)} %copy-done.6), custom_call_target="tpu_custom_call" | custom-call | tf_op jit(solution)/shard_map/pallas_call | solution.py:99
  76.8 7.1 %collective-permute-done.6 = bf16[8,18432]{1,0:T(8,128)(2,1)S(1)} collective-permute-done((bf16[8,18432]{1,0:T(8,128)(2,1)}, bf16[8,18432]{1,0:T(8,128)(2,1)S(1)}, u32[]{:S(2)}, u32[]{:S(2)}) %collective-permute-start.6) | collective-permute-done | bytes 294944 | tf_op jit(solution)/shard_map/ppermute | solution.py:30
  83.9 1.0 add.133.refs_4_
  85.1 6.8 %collective-permute-done.7.refs_5_ = bf16[8,18432]{1,0:T(8,128)(2,1)S(1)} collective-permute-done((bf16[8,18432]{1,0:T(8,128)(2,1)S(1)}, bf16[8,18432]{1,0:T(8,128)(2,1)S(1)}, u32[]{:S(2)}, u32[]{:S(2)}) %collective-permute-start.7) | collective-permute-done | bytes 294944 | tf_op jit(solution)/shard_map/ppermute | solution.py:258
  92.0 0.9 collective-permute-start.8
  92.9 4.3 %collective-permute-done.9.refs_6_ = bf16[8,9216]{1,0:T(8,128)(2,1)S(1)} collective-permute-done((bf16[8,9216]{1,0:T(8,128)(2,1)S(1)}, bf16[8,9216]{1,0:T(8,128)(2,1)S(1)}, u32[]{:S(2)}, u32[]{:S(2)}) %collective-permute-start.9) | collective-permute-done | bytes 147488 | tf_op jit(solution)/shard_map/ppermute | solution.py:266
  97.2 1.6 collective-permute-done.8.refs_7_
  98.8 3.6 %collective-permute-done.10.refs_8_ = bf16[8,9216]{1,0:T(8,128)(2,1)S(1)} collective-permute-done((bf16[8,9216]{1,0:T(8,128)(2,1)S(1)}, bf16[8,9216]{1,0:T(8,128)(2,1)S(1)}, u32[]{:S(2)}, u32[]{:S(2)}) %collective-permute-start.10) | collective-permute-done | bytes 147488 | tf_op jit(solution)/shard_map/ppermute | solution.py:266
  102.4 1.6 collective-permute-done.11.refs_9_
  104.0 3.6 %collective-permute-done.12.refs_10_ = bf16[8,9216]{1,0:T(8,128)(2,1)S(1)} collective-permute-done((bf16[8,9216]{1,0:T(8,128)(2,1)S(1)}, bf16[8,9216]{1,0:T(8,128)(2,1)S(1)}, u32[]{:S(2)}, u32[]{:S(2)}) %collective-permute-start.12) | collective-permute-done | bytes 147488 | tf_op jit(solution)/shard_map/ppermute | solution.py:266
  107.6 1.6 collective-permute-done.13.refs_11_
  109.2 3.6 %collective-permute-done.14.refs_12_ = bf16[8,9216]{1,0:T(8,128)(2,1)S(1)} collective-permute-done((bf16[8,9216]{1,0:T(8,128)(2,1)S(1)}, bf16[8,9216]{1,0:T(8,128)(2,1)S(1)}, u32[]{:S(2)}, u32[]{:S(2)}) %collective-permute-start.14) | collective-permute-done | bytes 147488 | tf_op jit(solution)/shard_map/ppermute | solution.py:266
  112.8 1.6 collective-permute-done.15.refs_13_
  114.4 3.6 %collective-permute-done.16.refs_14_ = bf16[8,9216]{1,0:T(8,128)(2,1)S(1)} collective-permute-done((bf16[8,9216]{1,0:T(8,128)(2,1)S(1)}, bf16[8,9216]{1,0:T(8,128)(2,1)S(1)}, u32[]{:S(2)}, u32[]{:S(2)}) %collective-permute-start.16) | collective-permute-done | bytes 147488 | tf_op jit(solution)/shard_map/ppermute | solution.py:266
  118.0 1.6 collective-permute-done.17.refs_15_
  119.6 3.6 %collective-permute-done.18.refs_16_ = bf16[8,9216]{1,0:T(8,128)(2,1)S(1)} collective-permute-done((bf16[8,9216]{1,0:T(8,128)(2,1)S(1)}, bf16[8,9216]{1,0:T(8,128)(2,1)S(1)}, u32[]{:S(2)}, u32[]{:S(2)}) %collective-permute-start.18) | collective-permute-done | bytes 147488 | tf_op jit(solution)/shard_map/ppermute | solution.py:266
  123.2 1.6 collective-permute-done.19.refs_17_
  124.8 3.6 %collective-permute-done.20.refs_18_ = bf16[8,9216]{1,0:T(8,128)(2,1)S(1)} collective-permute-done((bf16[8,9216]{1,0:T(8,128)(2,1)S(1)}, bf16[8,9216]{1,0:T(8,128)(2,1)S(1)}, u32[]{:S(2)}, u32[]{:S(2)}) %collective-permute-start.20) | collective-permute-done | bytes 147488 | tf_op jit(solution)/shard_map/ppermute | solution.py:266
  128.4 1.6 collective-permute-done.21.refs_19_
  130.0 3.6 %collective-permute-done.22.refs_20_ = bf16[8,9216]{1,0:T(8,128)(2,1)S(1)} collective-permute-done((bf16[8,9216]{1,0:T(8,128)(2,1)S(1)}, bf16[8,9216]{1,0:T(8,128)(2,1)S(1)}, u32[]{:S(2)}, u32[]{:S(2)}) %collective-permute-start.22) | collective-permute-done | bytes 147488 | tf_op jit(solution)/shard_map/ppermute | solution.py:266
  133.7 1.6 collective-permute-done.23.refs_21_
  135.2 3.6 %collective-permute-done.24.refs_22_ = bf16[8,9216]{1,0:T(8,128)(2,1)S(1)} collective-permute-done((bf16[8,9216]{1,0:T(8,128)(2,1)S(1)}, bf16[8,9216]{1,0:T(8,128)(2,1)S(1)}, u32[]{:S(2)}, u32[]{:S(2)}) %collective-permute-start.24) | collective-permute-done | bytes 147488 | tf_op jit(solution)/shard_map/ppermute | solution.py:266
  138.9 1.6 collective-permute-done.25.refs_23_
  140.4 3.6 %collective-permute-done.26.refs_24_ = bf16[8,9216]{1,0:T(8,128)(2,1)S(1)} collective-permute-done((bf16[8,9216]{1,0:T(8,128)(2,1)S(1)}, bf16[8,9216]{1,0:T(8,128)(2,1)S(1)}, u32[]{:S(2)}, u32[]{:S(2)}) %collective-permute-start.26) | collective-permute-done | bytes 147488 | tf_op jit(solution)/shard_map/ppermute | solution.py:266
  144.1 1.6 collective-permute-done.27.refs_25_
  145.6 3.6 %collective-permute-done.28.refs_26_ = bf16[8,9216]{1,0:T(8,128)(2,1)S(1)} collective-permute-done((bf16[8,9216]{1,0:T(8,128)(2,1)S(1)}, bf16[8,9216]{1,0:T(8,128)(2,1)S(1)}, u32[]{:S(2)}, u32[]{:S(2)}) %collective-permute-start.28) | collective-permute-done | bytes 147488 | tf_op jit(solution)/shard_map/ppermute | solution.py:266
  149.3 1.6 collective-permute-done.29.refs_27_
  150.9 3.6 %collective-permute-done.30.refs_28_ = bf16[8,9216]{1,0:T(8,128)(2,1)S(1)} collective-permute-done((bf16[8,9216]{1,0:T(8,128)(2,1)S(1)}, bf16[8,9216]{1,0:T(8,128)(2,1)S(1)}, u32[]{:S(2)}, u32[]{:S(2)}) %collective-permute-start.30) | collective-permute-done | bytes 147488 | tf_op jit(solution)/shard_map/ppermute | solution.py:266
  154.5 1.6 collective-permute-done.31.refs_29_
  156.1 3.6 %collective-permute-done.32.refs_30_ = bf16[8,9216]{1,0:T(8,128)(2,1)S(1)} collective-permute-done((bf16[8,9216]{1,0:T(8,128)(2,1)S(1)}, bf16[8,9216]{1,0:T(8,128)(2,1)S(1)}, u32[]{:S(2)}, u32[]{:S(2)}) %collective-permute-start.32) | collective-permute-done | bytes 147488 | tf_op jit(solution)/shard_map/ppermute | solution.py:266
  159.7 1.6 collective-permute-done.33.refs_31_
  161.7 16.5 %collective-permute-start.5 = (bf16[256,4096]{1,0:T(8,128)(2,1)S(1)}, bf16[256,4096]{1,0:T(8,128)(2,1)S(1)}, u32[]{:S(2)}, u32[]{:S(2)}) collective-permute-start(bf16[256,4096]{1,0:T(8,128)(2,1)S(1)} %copy-done), channel_id=1, source_target_pairs={{0,1},{1,0},{2,3},{3,2},{4,5},{5,4},{6,7},{7,6},{8,9},{9,8},{10,11... | collective-permute-start | bytes 6291464 | tf_op jit(solution)/shard_map/ppermute | solution.py:30
  179.3 1.3 slice.95
  181.2 0.8 collective-permute-done.5.refs_3_
  182.0 1.4 copy-done.1
  183.4 1.8 collective-permute-done.36.refs_34_
  185.9 15.5 %shard_map.67 = f32[8,8]{1,0:T(8,128)S(1)} custom-call(s32[4]{0:T(128)} %pad_add_fusion.1.lens_ref, s32[2]{0:T(128)} %pad_add_fusion.seat_ref, s32[2]{0:T(128)} %get-tuple-element.412.routed_ref, bf16[256,14336]{1,0:T(8,128)(2,1)} %refs_0_.1, bf16[256,14336]{1,0:T(8,128)(2,1)} %collective-permute-done.4.refs_1_, bf16[256,4096]{1,0:T(8,128)(2,1)S(1)} %copy-done, ...), custom_call_target="tpu_custom_call" | custom-call | tf_op jit(solution)/shard_map/pallas_call | solution.py:187
  201.5 3.7 %collective-permute-start.37 = (f32[2,8]{1,0:T(2,128)S(1)}, f32[2,8]{1,0:T(2,128)S(1)}, u32[]{:S(2)}, u32[]{:S(2)}) collective-permute-start(f32[2,8]{1,0:T(2,128)S(1)} %slice.100), channel_id=1, source_target_pairs={{0,1},{1,0},{2,3},{3,2},{4,5},{5,4},{6,7},{7,6},{8,9},{9,8},{10,11... | collective-permute-start | bytes 200 | tf_op jit(solution)/shard_map/ppermute | solution.py:30
  205.2 0.8 collective-permute-done.37
  (133 shorter events, 4.5 us)
Async XLA Ops:
  3.6 22.0 %collective-permute-start.1 = (bf16[24,9344]{1,0:T(8,128)(2,1)S(1)}, bf16[24,9344]{1,0:T(8,128)(2,1)S(1)}, u32[]{:S(2)}, u32[]{:S(2)}) collective-permute-start(bf16[24,9344]{1,0:T(8,128)(2,1)S(1)} %maximum_maximum_fusion), channel_id=1, source_target_pairs={{0,1},{1,0},{2,3},{3,2},{4,5},{5,4},{6,7},{7,6},{8,9},{9,8},{10,11... | collective-permute-start | bytes 1345544 | tf_op jit(solution)/shard_map/ppermute | solution.py:30
  28.7 132.9 %copy-start.34 = (s32[2]{0:T(128)S(1)}, s32[2]{0:T(128)}, u32[]{:S(2)}) copy-start(s32[2]{0:T(128)} %param.12) | copy-start | bytes 28
  28.7 132.9 %copy-start = (bf16[256,4096]{1,0:T(8,128)(2,1)S(1)}, bf16[256,4096]{1,0:T(8,128)(2,1)}, u32[]{:S(2)}) copy-start(bf16[256,4096]{1,0:T(8,128)(2,1)} %refs_2_.1) | copy-start | bytes 6291460
  28.7 31.1 %collective-permute-start.2 = (bf16[16,18432]{1,0:T(8,128)(2,1)S(1)}, bf16[16,18432]{1,0:T(8,128)(2,1)}, u32[]{:S(2)}, u32[]{:S(2)}) collective-permute-start(bf16[16,18432]{1,0:T(8,128)(2,1)S(1)} %convolution_convert_fusion), channel_id=1, source_target_pairs={{1,3},{3,5},{5,7},{7,9},{9,11},{11,13},{13,15},{15,17},{17,19},{19... | collective-permute-start | bytes 1769480 | tf_op jit(solution)/shard_map/ppermute | solution.py:244
  28.9 30.9 %collective-permute-start.3 = (bf16[8,18432]{1,0:T(8,128)(2,1)S(1)}, bf16[8,18432]{1,0:T(8,128)(2,1)S(1)}, u32[]{:S(2)}, u32[]{:S(2)}) collective-permute-start(bf16[8,18432]{1,0:T(8,128)(2,1)S(1)} %slice_select_fusion), channel_id=1, source_target_pairs={{1,5},{3,7},{5,9},{7,11},{9,13},{11,15},{13,17},{15,19},{17,21},{1... | collective-permute-start | bytes 884744 | tf_op jit(solution)/shard_map/ppermute | solution.py:245
  59.9 125.3 %collective-permute-start.4 = (bf16[256,14336]{1,0:T(8,128)(2,1)}, bf16[256,14336]{1,0:T(8,128)(2,1)}, u32[]{:S(2)}, u32[]{:S(2)}) collective-permute-start(bf16[256,14336]{1,0:T(8,128)(2,1)} %refs_0_.1), channel_id=1, source_target_pairs={{0,1},{1,0},{2,3},{3,2},{4,5},{5,4},{6,7},{7,6},{8,9},{9,8},{10,11... | collective-permute-start | bytes 22020104 | tf_op jit(solution)/shard_map/ppermute | solution.py:30
  76.7 7.2 %collective-permute-start.6 = (bf16[8,18432]{1,0:T(8,128)(2,1)}, bf16[8,18432]{1,0:T(8,128)(2,1)S(1)}, u32[]{:S(2)}, u32[]{:S(2)}) collective-permute-start(bf16[8,18432]{1,0:T(8,128)(2,1)} %get-tuple-element.415), channel_id=1, source_target_pairs={{0,1},{1,0},{2,3},{3,2},{4,5},{5,4},{6,7},{7,6},{8,9},{9,8},{10,11... | collective-permute-start | bytes 884744 | tf_op jit(solution)/shard_map/ppermute | solution.py:30
  84.9 100.3 %copy-start.2 = (bf16[8,18432]{1,0:T(8,128)(2,1)}, bf16[8,18432]{1,0:T(8,128)(2,1)S(1)}, u32[]{:S(2)}) copy-start(bf16[8,18432]{1,0:T(8,128)(2,1)S(1)} %add.133.refs_4_) | copy-start | bytes 884740
  85.0 6.9 %collective-permute-start.7 = (bf16[8,18432]{1,0:T(8,128)(2,1)S(1)}, bf16[8,18432]{1,0:T(8,128)(2,1)S(1)}, u32[]{:S(2)}, u32[]{:S(2)}) collective-permute-start(bf16[8,18432]{1,0:T(8,128)(2,1)S(1)} %add.133.refs_4_), channel_id=1, source_target_pairs={{1,3},{3,5},{5,7},{7,9},{9,11},{11,13},{13,15},{15,17},{17,19},{19... | collective-permute-start | bytes 884744 | tf_op jit(solution)/shard_map/ppermute | solution.py:258
  91.9 93.4 %copy-start.3 = (bf16[8,18432]{1,0:T(8,128)(2,1)}, bf16[8,18432]{1,0:T(8,128)(2,1)S(1)}, u32[]{:S(2)}) copy-start(bf16[8,18432]{1,0:T(8,128)(2,1)S(1)} %collective-permute-done.7.refs_5_) | copy-start | bytes 884740
  91.9 5.3 %collective-permute-start.9 = (bf16[8,9216]{1,0:T(8,128)(2,1)S(1)}, bf16[8,9216]{1,0:T(8,128)(2,1)S(1)}, u32[]{:S(2)}, u32[]{:S(2)}) collective-permute-start(bf16[8,9216]{1,0:T(8,128)(2,1)S(1)} %get-tuple-element.585), channel_id=1, source_target_pairs={{1,3},{3,5},{5,7},{7,9},{9,11},{11,13},{13,15},{15,17},{17,19},{19... | collective-permute-start | bytes 442376 | tf_op jit(solution)/shard_map/ppermute | solution.py:266
  92.0 6.8 %collective-permute-start.8 = (bf16[8,9216]{1,0:T(8,128)(2,1)S(1)}, bf16[8,9216]{1,0:T(8,128)(2,1)S(1)}, u32[]{:S(2)}, u32[]{:S(2)}) collective-permute-start(bf16[8,9216]{1,0:T(8,128)(2,1)S(1)} %get-tuple-element.586), channel_id=1, source_target_pairs={{1,3},{3,5},{5,7},{7,9},{9,11},{11,13},{13,15},{15,17},{17,19},{19... | collective-permute-start | bytes 442376 | tf_op jit(solution)/shard_map/ppermute | solution.py:266
  97.2 88.0 %copy-start.8 = (bf16[8,9216]{1,0:T(8,128)(2,1)}, bf16[8,9216]{1,0:T(8,128)(2,1)S(1)}, u32[]{:S(2)}) copy-start(bf16[8,9216]{1,0:T(8,128)(2,1)S(1)} %collective-permute-done.9.refs_6_) | copy-start | bytes 442372
  97.2 5.2 %collective-permute-start.10 = (bf16[8,9216]{1,0:T(8,128)(2,1)S(1)}, bf16[8,9216]{1,0:T(8,128)(2,1)S(1)}, u32[]{:S(2)}, u32[]{:S(2)}) collective-permute-start(bf16[8,9216]{1,0:T(8,128)(2,1)S(1)} %collective-permute-done.9.refs_6_), channel_id=1, source_target_pairs={{1,3},{3,5},{5,7},{7,9},{9,11},{11,13},{13,15},{15,17},{17,19},{19... | collective-permute-start | bytes 442376 | tf_op jit(solution)/shard_map/ppermute | solution.py:266
  98.8 79.5 %copy-start.9 = (bf16[8,9216]{1,0:T(8,128)(2,1)}, bf16[8,9216]{1,0:T(8,128)(2,1)S(1)}, u32[]{:S(2)}) copy-start(bf16[8,9216]{1,0:T(8,128)(2,1)S(1)} %collective-permute-done.8.refs_7_) | copy-start | bytes 442372
  98.8 5.2 %collective-permute-start.11 = (bf16[8,9216]{1,0:T(8,128)(2,1)S(1)}, bf16[8,9216]{1,0:T(8,128)(2,1)S(1)}, u32[]{:S(2)}, u32[]{:S(2)}) collective-permute-start(bf16[8,9216]{1,0:T(8,128)(2,1)S(1)} %collective-permute-done.8.refs_7_), channel_id=1, source_target_pairs={{1,3},{3,5},{5,7},{7,9},{9,11},{11,13},{13,15},{15,17},{17,19},{19... | collective-permute-start | bytes 442376 | tf_op jit(solution)/shard_map/ppermute | solution.py:266
  102.4 57.3 %copy-start.10 = (bf16[8,9216]{1,0:T(8,128)(2,1)}, bf16[8,9216]{1,0:T(8,128)(2,1)S(1)}, u32[]{:S(2)}) copy-start(bf16[8,9216]{1,0:T(8,128)(2,1)S(1)} %collective-permute-done.10.refs_8_) | copy-start | bytes 442372
  102.4 5.2 %collective-permute-start.12 = (bf16[8,9216]{1,0:T(8,128)(2,1)S(1)}, bf16[8,9216]{1,0:T(8,128)(2,1)S(1)}, u32[]{:S(2)}, u32[]{:S(2)}) collective-permute-start(bf16[8,9216]{1,0:T(8,128)(2,1)S(1)} %collective-permute-done.10.refs_8_), channel_id=1, source_target_pairs={{1,3},{3,5},{5,7},{7,9},{9,11},{11,13},{13,15},{15,17},{17,19},{19... | collective-permute-start | bytes 442376 | tf_op jit(solution)/shard_map/ppermute | solution.py:266
  104.0 52.1 %copy-start.11 = (bf16[8,9216]{1,0:T(8,128)(2,1)}, bf16[8,9216]{1,0:T(8,128)(2,1)S(1)}, u32[]{:S(2)}) copy-start(bf16[8,9216]{1,0:T(8,128)(2,1)S(1)} %collective-permute-done.11.refs_9_) | copy-start | bytes 442372
  104.0 5.2 %collective-permute-start.13 = (bf16[8,9216]{1,0:T(8,128)(2,1)S(1)}, bf16[8,9216]{1,0:T(8,128)(2,1)S(1)}, u32[]{:S(2)}, u32[]{:S(2)}) collective-permute-start(bf16[8,9216]{1,0:T(8,128)(2,1)S(1)} %collective-permute-done.11.refs_9_), channel_id=1, source_target_pairs={{1,3},{3,5},{5,7},{7,9},{9,11},{11,13},{13,15},{15,17},{17,19},{19... | collective-permute-start | bytes 442376 | tf_op jit(solution)/shard_map/ppermute | solution.py:266
  107.6 70.6 %copy-start.12 = (bf16[8,9216]{1,0:T(8,128)(2,1)}, bf16[8,9216]{1,0:T(8,128)(2,1)S(1)}, u32[]{:S(2)}) copy-start(bf16[8,9216]{1,0:T(8,128)(2,1)S(1)} %collective-permute-done.12.refs_10_) | copy-start | bytes 442372
  107.6 5.2 %collective-permute-start.14 = (bf16[8,9216]{1,0:T(8,128)(2,1)S(1)}, bf16[8,9216]{1,0:T(8,128)(2,1)S(1)}, u32[]{:S(2)}, u32[]{:S(2)}) collective-permute-start(bf16[8,9216]{1,0:T(8,128)(2,1)S(1)} %collective-permute-done.12.refs_10_), channel_id=1, source_target_pairs={{1,3},{3,5},{5,7},{7,9},{9,11},{11,13},{13,15},{15,17},{17,19},{19... | collective-permute-start | bytes 442376 | tf_op jit(solution)/shard_map/ppermute | solution.py:266
  109.2 52.1 %copy-start.13 = (bf16[8,9216]{1,0:T(8,128)(2,1)}, bf16[8,9216]{1,0:T(8,128)(2,1)S(1)}, u32[]{:S(2)}) copy-start(bf16[8,9216]{1,0:T(8,128)(2,1)S(1)} %collective-permute-done.13.refs_11_) | copy-start | bytes 442372
  109.2 5.2 %collective-permute-start.15 = (bf16[8,9216]{1,0:T(8,128)(2,1)S(1)}, bf16[8,9216]{1,0:T(8,128)(2,1)S(1)}, u32[]{:S(2)}, u32[]{:S(2)}) collective-permute-start(bf16[8,9216]{1,0:T(8,128)(2,1)S(1)} %collective-permute-done.13.refs_11_), channel_id=1, source_target_pairs={{1,3},{3,5},{5,7},{7,9},{9,11},{11,13},{13,15},{15,17},{17,19},{19... | collective-permute-start | bytes 442376 | tf_op jit(solution)/shard_map/ppermute | solution.py:266
  112.8 48.4 %copy-start.14 = (bf16[8,9216]{1,0:T(8,128)(2,1)}, bf16[8,9216]{1,0:T(8,128)(2,1)S(1)}, u32[]{:S(2)}) copy-start(bf16[8,9216]{1,0:T(8,128)(2,1)S(1)} %collective-permute-done.14.refs_12_) | copy-start | bytes 442372
  112.8 5.2 %collective-permute-start.16 = (bf16[8,9216]{1,0:T(8,128)(2,1)S(1)}, bf16[8,9216]{1,0:T(8,128)(2,1)S(1)}, u32[]{:S(2)}, u32[]{:S(2)}) collective-permute-start(bf16[8,9216]{1,0:T(8,128)(2,1)S(1)} %collective-permute-done.14.refs_12_), channel_id=1, source_target_pairs={{1,3},{3,5},{5,7},{7,9},{9,11},{11,13},{13,15},{15,17},{17,19},{19... | collective-permute-start | bytes 442376 | tf_op jit(solution)/shard_map/ppermute | solution.py:266
  114.4 5.2 %collective-permute-start.17 = (bf16[8,9216]{1,0:T(8,128)(2,1)S(1)}, bf16[8,9216]{1,0:T(8,128)(2,1)S(1)}, u32[]{:S(2)}, u32[]{:S(2)}) collective-permute-start(bf16[8,9216]{1,0:T(8,128)(2,1)S(1)} %collective-permute-done.15.refs_13_), channel_id=1, source_target_pairs={{1,3},{3,5},{5,7},{7,9},{9,11},{11,13},{13,15},{15,17},{17,19},{19... | collective-permute-start | bytes 442376 | tf_op jit(solution)/shard_map/ppermute | solution.py:266
  118.0 5.2 %collective-permute-start.18 = (bf16[8,9216]{1,0:T(8,128)(2,1)S(1)}, bf16[8,9216]{1,0:T(8,128)(2,1)S(1)}, u32[]{:S(2)}, u32[]{:S(2)}) collective-permute-start(bf16[8,9216]{1,0:T(8,128)(2,1)S(1)} %collective-permute-done.16.refs_14_), channel_id=1, source_target_pairs={{1,3},{3,5},{5,7},{7,9},{9,11},{11,13},{13,15},{15,17},{17,19},{19... | collective-permute-start | bytes 442376 | tf_op jit(solution)/shard_map/ppermute | solution.py:266
  119.6 5.2 %collective-permute-start.19 = (bf16[8,9216]{1,0:T(8,128)(2,1)S(1)}, bf16[8,9216]{1,0:T(8,128)(2,1)S(1)}, u32[]{:S(2)}, u32[]{:S(2)}) collective-permute-start(bf16[8,9216]{1,0:T(8,128)(2,1)S(1)} %collective-permute-done.17.refs_15_), channel_id=1, source_target_pairs={{1,3},{3,5},{5,7},{7,9},{9,11},{11,13},{13,15},{15,17},{17,19},{19... | collective-permute-start | bytes 442376 | tf_op jit(solution)/shard_map/ppermute | solution.py:266
  123.2 5.2 %collective-permute-start.20 = (bf16[8,9216]{1,0:T(8,128)(2,1)S(1)}, bf16[8,9216]{1,0:T(8,128)(2,1)S(1)}, u32[]{:S(2)}, u32[]{:S(2)}) collective-permute-start(bf16[8,9216]{1,0:T(8,128)(2,1)S(1)} %collective-permute-done.18.refs_16_), channel_id=1, source_target_pairs={{1,3},{3,5},{5,7},{7,9},{9,11},{11,13},{13,15},{15,17},{17,19},{19... | collective-permute-start | bytes 442376 | tf_op jit(solution)/shard_map/ppermute | solution.py:266
  124.8 5.2 %collective-permute-start.21 = (bf16[8,9216]{1,0:T(8,128)(2,1)S(1)}, bf16[8,9216]{1,0:T(8,128)(2,1)S(1)}, u32[]{:S(2)}, u32[]{:S(2)}) collective-permute-start(bf16[8,9216]{1,0:T(8,128)(2,1)S(1)} %collective-permute-done.19.refs_17_), channel_id=1, source_target_pairs={{1,3},{3,5},{5,7},{7,9},{9,11},{11,13},{13,15},{15,17},{17,19},{19... | collective-permute-start | bytes 442376 | tf_op jit(solution)/shard_map/ppermute | solution.py:266
  128.4 5.2 %collective-permute-start.22 = (bf16[8,9216]{1,0:T(8,128)(2,1)S(1)}, bf16[8,9216]{1,0:T(8,128)(2,1)S(1)}, u32[]{:S(2)}, u32[]{:S(2)}) collective-permute-start(bf16[8,9216]{1,0:T(8,128)(2,1)S(1)} %collective-permute-done.20.refs_18_), channel_id=1, source_target_pairs={{1,3},{3,5},{5,7},{7,9},{9,11},{11,13},{13,15},{15,17},{17,19},{19... | collective-permute-start | bytes 442376 | tf_op jit(solution)/shard_map/ppermute | solution.py:266
  130.0 5.2 %collective-permute-start.23 = (bf16[8,9216]{1,0:T(8,128)(2,1)S(1)}, bf16[8,9216]{1,0:T(8,128)(2,1)S(1)}, u32[]{:S(2)}, u32[]{:S(2)}) collective-permute-start(bf16[8,9216]{1,0:T(8,128)(2,1)S(1)} %collective-permute-done.21.refs_19_), channel_id=1, source_target_pairs={{1,3},{3,5},{5,7},{7,9},{9,11},{11,13},{13,15},{15,17},{17,19},{19... | collective-permute-start | bytes 442376 | tf_op jit(solution)/shard_map/ppermute | solution.py:266
  133.6 5.2 %collective-permute-start.24 = (bf16[8,9216]{1,0:T(8,128)(2,1)S(1)}, bf16[8,9216]{1,0:T(8,128)(2,1)S(1)}, u32[]{:S(2)}, u32[]{:S(2)}) collective-permute-start(bf16[8,9216]{1,0:T(8,128)(2,1)S(1)} %collective-permute-done.22.refs_20_), channel_id=1, source_target_pairs={{1,3},{3,5},{5,7},{7,9},{9,11},{11,13},{13,15},{15,17},{17,19},{19... | collective-permute-start | bytes 442376 | tf_op jit(solution)/shard_map/ppermute | solution.py:266
  135.2 5.2 %collective-permute-start.25 = (bf16[8,9216]{1,0:T(8,128)(2,1)S(1)}, bf16[8,9216]{1,0:T(8,128)(2,1)S(1)}, u32[]{:S(2)}, u32[]{:S(2)}) collective-permute-start(bf16[8,9216]{1,0:T(8,128)(2,1)S(1)} %collective-permute-done.23.refs_21_), channel_id=1, source_target_pairs={{1,3},{3,5},{5,7},{7,9},{9,11},{11,13},{13,15},{15,17},{17,19},{19... | collective-permute-start | bytes 442376 | tf_op jit(solution)/shard_map/ppermute | solution.py:266
  138.9 5.2 %collective-permute-start.26 = (bf16[8,9216]{1,0:T(8,128)(2,1)S(1)}, bf16[8,9216]{1,0:T(8,128)(2,1)S(1)}, u32[]{:S(2)}, u32[]{:S(2)}) collective-permute-start(bf16[8,9216]{1,0:T(8,128)(2,1)S(1)} %collective-permute-done.24.refs_22_), channel_id=1, source_target_pairs={{1,3},{3,5},{5,7},{7,9},{9,11},{11,13},{13,15},{15,17},{17,19},{19... | collective-permute-start | bytes 442376 | tf_op jit(solution)/shard_map/ppermute | solution.py:266
  140.4 5.2 %collective-permute-start.27 = (bf16[8,9216]{1,0:T(8,128)(2,1)S(1)}, bf16[8,9216]{1,0:T(8,128)(2,1)S(1)}, u32[]{:S(2)}, u32[]{:S(2)}) collective-permute-start(bf16[8,9216]{1,0:T(8,128)(2,1)S(1)} %collective-permute-done.25.refs_23_), channel_id=1, source_target_pairs={{1,3},{3,5},{5,7},{7,9},{9,11},{11,13},{13,15},{15,17},{17,19},{19... | collective-permute-start | bytes 442376 | tf_op jit(solution)/shard_map/ppermute | solution.py:266
  144.1 5.2 %collective-permute-start.28 = (bf16[8,9216]{1,0:T(8,128)(2,1)S(1)}, bf16[8,9216]{1,0:T(8,128)(2,1)S(1)}, u32[]{:S(2)}, u32[]{:S(2)}) collective-permute-start(bf16[8,9216]{1,0:T(8,128)(2,1)S(1)} %collective-permute-done.26.refs_24_), channel_id=1, source_target_pairs={{1,3},{3,5},{5,7},{7,9},{9,11},{11,13},{13,15},{15,17},{17,19},{19... | collective-permute-start | bytes 442376 | tf_op jit(solution)/shard_map/ppermute | solution.py:266
  145.6 5.2 %collective-permute-start.29 = (bf16[8,9216]{1,0:T(8,128)(2,1)S(1)}, bf16[8,9216]{1,0:T(8,128)(2,1)S(1)}, u32[]{:S(2)}, u32[]{:S(2)}) collective-permute-start(bf16[8,9216]{1,0:T(8,128)(2,1)S(1)} %collective-permute-done.27.refs_25_), channel_id=1, source_target_pairs={{1,3},{3,5},{5,7},{7,9},{9,11},{11,13},{13,15},{15,17},{17,19},{19... | collective-permute-start | bytes 442376 | tf_op jit(solution)/shard_map/ppermute | solution.py:266
  149.3 5.2 %collective-permute-start.30 = (bf16[8,9216]{1,0:T(8,128)(2,1)S(1)}, bf16[8,9216]{1,0:T(8,128)(2,1)S(1)}, u32[]{:S(2)}, u32[]{:S(2)}) collective-permute-start(bf16[8,9216]{1,0:T(8,128)(2,1)S(1)} %collective-permute-done.28.refs_26_), channel_id=1, source_target_pairs={{1,3},{3,5},{5,7},{7,9},{9,11},{11,13},{13,15},{15,17},{17,19},{19... | collective-permute-start | bytes 442376 | tf_op jit(solution)/shard_map/ppermute | solution.py:266
  150.8 5.2 %collective-permute-start.31 = (bf16[8,9216]{1,0:T(8,128)(2,1)S(1)}, bf16[8,9216]{1,0:T(8,128)(2,1)S(1)}, u32[]{:S(2)}, u32[]{:S(2)}) collective-permute-start(bf16[8,9216]{1,0:T(8,128)(2,1)S(1)} %collective-permute-done.29.refs_27_), channel_id=1, source_target_pairs={{1,3},{3,5},{5,7},{7,9},{9,11},{11,13},{13,15},{15,17},{17,19},{19... | collective-permute-start | bytes 442376 | tf_op jit(solution)/shard_map/ppermute | solution.py:266
  154.5 5.2 %collective-permute-start.32 = (bf16[8,9216]{1,0:T(8,128)(2,1)S(1)}, bf16[8,9216]{1,0:T(8,128)(2,1)S(1)}, u32[]{:S(2)}, u32[]{:S(2)}) collective-permute-start(bf16[8,9216]{1,0:T(8,128)(2,1)S(1)} %collective-permute-done.30.refs_28_), channel_id=1, source_target_pairs={{1,3},{3,5},{5,7},{7,9},{9,11},{11,13},{13,15},{15,17},{17,19},{19... | collective-permute-start | bytes 442376 | tf_op jit(solution)/shard_map/ppermute | solution.py:266
  156.1 5.2 %collective-permute-start.33 = (bf16[8,9216]{1,0:T(8,128)(2,1)S(1)}, bf16[8,9216]{1,0:T(8,128)(2,1)S(1)}, u32[]{:S(2)}, u32[]{:S(2)}) collective-permute-start(bf16[8,9216]{1,0:T(8,128)(2,1)S(1)} %collective-permute-done.31.refs_29_), channel_id=1, source_target_pairs={{1,3},{3,5},{5,7},{7,9},{9,11},{11,13},{13,15},{15,17},{17,19},{19... | collective-permute-start | bytes 442376 | tf_op jit(solution)/shard_map/ppermute | solution.py:266
  159.7 18.6 %collective-permute-start.34 = (bf16[8,9216]{1,0:T(8,128)(2,1)S(1)}, bf16[8,9216]{1,0:T(8,128)(2,1)S(1)}, u32[]{:S(2)}, u32[]{:S(2)}) collective-permute-start(bf16[8,9216]{1,0:T(8,128)(2,1)S(1)} %collective-permute-done.32.refs_30_), channel_id=1, source_target_pairs={{1,3},{3,5},{5,7},{7,9},{9,11},{11,13},{13,15},{15,17},{17,19},{19... | collective-permute-start | bytes 442376 | tf_op jit(solution)/shard_map/ppermute | solution.py:266
  161.4 16.8 %collective-permute-start.35 = (bf16[8,9216]{1,0:T(8,128)(2,1)S(1)}, bf16[8,9216]{1,0:T(8,128)(2,1)S(1)}, u32[]{:S(2)}, u32[]{:S(2)}) collective-permute-start(bf16[8,9216]{1,0:T(8,128)(2,1)S(1)} %collective-permute-done.33.refs_31_), channel_id=1, source_target_pairs={{1,3},{3,5},{5,7},{7,9},{9,11},{11,13},{13,15},{15,17},{17,19},{19... | collective-permute-start | bytes 442376 | tf_op jit(solution)/shard_map/ppermute | solution.py:266
  161.7 20.3 %collective-permute-start.5 = (bf16[256,4096]{1,0:T(8,128)(2,1)S(1)}, bf16[256,4096]{1,0:T(8,128)(2,1)S(1)}, u32[]{:S(2)}, u32[]{:S(2)}) collective-permute-start(bf16[256,4096]{1,0:T(8,128)(2,1)S(1)} %copy-done), channel_id=1, source_target_pairs={{0,1},{1,0},{2,3},{3,2},{4,5},{5,4},{6,7},{7,6},{8,9},{9,8},{10,11... | collective-permute-start | bytes 6291464 | tf_op jit(solution)/shard_map/ppermute | solution.py:30
  178.3 6.9 %collective-permute-start.36 = (bf16[8,18432]{1,0:T(8,128)(2,1)S(1)}, bf16[8,18432]{1,0:T(8,128)(2,1)S(1)}, u32[]{:S(2)}, u32[]{:S(2)}) collective-permute-start(bf16[8,18432]{1,0:T(8,128)(2,1)S(1)} %pad_maximum_fusion.2), channel_id=1, source_target_pairs={{1,3},{3,5},{5,7},{7,9},{9,11},{11,13},{13,15},{15,17},{17,19},{19... | collective-permute-start | bytes 884744 | tf_op jit(solution)/shard_map/ppermute | solution.py:267
  201.5 4.6 %collective-permute-start.37 = (f32[2,8]{1,0:T(2,128)S(1)}, f32[2,8]{1,0:T(2,128)S(1)}, u32[]{:S(2)}, u32[]{:S(2)}) collective-permute-start(f32[2,8]{1,0:T(2,128)S(1)} %slice.100), channel_id=1, source_target_pairs={{0,1},{1,0},{2,3},{3,2},{4,5},{5,4},{6,7},{7,6},{8,9},{9,8},{10,11... | collective-permute-start | bytes 200 | tf_op jit(solution)/shard_map/ppermute | solution.py:30
  (26 other events, 504.0 us)

commit v2 on v1

--- a/solution.py
+++ b/solution.py
@@ -246,11 +246,11 @@
     held_here = jnp.where(device_list == 2 * z, n0, jnp.where(device_list == 2 * z + 1, n1, 0))
     counts = lax.psum(held_here, "z")
     one_hop, two_hops, counts = lax.optimization_barrier((one_hop, two_hops, counts))
-    counts, grads_t, inputs_t = lax.optimization_barrier((counts, grads, inputs))
-    grads_s, inputs_s = swap(grads_t), swap(inputs_t)
     seat = jnp.stack([z, core]).astype(jnp.int32)
     mine, routed = routed_rows(raw, one_hop, two_hops, counts, seat, block)
     mine = mine + swap(mine)
+    mine, grads_t, inputs_t = lax.optimization_barrier((mine, grads, inputs))
+    grads_s, inputs_s = swap(grads_t), swap(inputs_t)
 
     steps = chips // 2
     piece = width // CHAINS

time: 207 us -> 201 us (0.971)
  waiting for transfers between devices: 86.9 us -> 81.3 us
    ppermute x5, waiting for transfers between devices: 10.1 us -> 4.47 us  [swap(): return lax.ppermute(x, 'core', [(0, 1), (1, 0)])]
  transfers between devices with their start and end apart: 37 -> 37, of which waited for: 32 -> 32; matrix products, arithmetic and copies ran while one was open for 2% -> 1% of each run, Pallas kernels for 2% -> 0%
where the time goes in v2:
time: 201 us
  waiting for transfers between devices  81.3 us (40%)
  starting transfers between devices  54.8 us (27%)
  blocking collectives  30.2 us (15%)
  Pallas kernels  19.7 us (10%)
  local copies, waits for them, and re-layouts  6.98 us (3%)
  other arithmetic  4.63 us (2%)
    ppermute x28, waiting for transfers between devices, on_device(): chain.append(lax.ppermute(chain[k], PART, forth))  68.2 us
    ppermute x5, starting transfers between devices, swap(): return lax.ppermute(x, 'core', [(0, 1), (1, 0)])  53.1 us
    psum x1, blocking collectives, on_device(): counts = lax.psum(held_here, 'z')  30.2 us
    pallas_call x1, Pallas kernels, scored(): pl.pallas_call(body, out_shape=jax.ShapeDtypeStruct((8, queries), jnp.flo...  15.6 us
    ppermute x1, waiting for transfers between devices, on_device(): near = lax.ppermute(mine, PART, forth)  6.78 us
    unnamed x73, local copies, waits for them, and re-layouts  4.57 us
    ppermute x5, waiting for transfers between devices, swap(): return lax.ppermute(x, 'core', [(0, 1), (1, 0)])  4.47 us
    pallas_call x1, Pallas kernels, routed_rows(): pl.pallas_call(body, out_shape=(jax.ShapeDtypeStruct((block, width), jnp....  4.14 us
  transfers between devices with their start and end apart: 37, of which 32 were waited for; matrix products, arithmetic and copies ran while one was open for 1% of the time, Pallas kernels for 0%

profile of v2, /device:TPU:37, one launch (start us, length us, event | category | flops | bytes accessed | tf_op | source)
XLA Modules:
  0.0 201.0 jit_solution(1965525808323306361)
XLA Ops:
  0.0 1.1 constant_dynamic-update-slice_fusion.1
  2.4 0.9 constant_dynamic-update-slice_fusion
  3.6 20.5 %collective-permute-start.1 = (bf16[24,9344]{1,0:T(8,128)(2,1)S(1)}, bf16[24,9344]{1,0:T(8,128)(2,1)S(1)}, u32[]{:S(2)}, u32[]{:S(2)}) collective-permute-start(bf16[24,9344]{1,0:T(8,128)(2,1)S(1)} %maximum_maximum_fusion), channel_id=1, source_target_pairs={{0,1},{1,0},{2,3},{3,2},{4,5},{5,4},{6,7},{7,6},{8,9},{9,8},{10,11... | collective-permute-start | bytes 1345544 | tf_op jit(solution)/shard_map/ppermute | solution.py:30
  24.2 1.4 collective-permute-done.1
  26.0 1.1 pad_maximum_fusion.raw_ref
  27.2 1.5 convolution_convert_fusion
  29.7 30.2 %psum.7.counts_ref = s32[64]{0:T(128)S(1)} all-reduce(s32[64]{0:T(128)S(1)} %compare_select_fusion.4), channel_id=1, replica_groups=mesh['groups'=4,'z'=32,'core'=2] {'z'}, use_global_device_ids=true, to_apply=%region_0.1 | all-reduce | flops 64 | bytes 512 | tf_op jit(solution)/shard_map/psum | solution.py:247
  59.9 0.7 copy-done.6
  60.6 4.1 %shard_map.66 = (bf16[8,18432]{1,0:T(8,128)(2,1)}, s32[2]{0:T(128)}) custom-call(s32[64]{0:T(128)S(1)} %psum.7.counts_ref, s32[2]{0:T(128)} %pad_add_fusion.seat_ref, bf16[24,18432]{1,0:T(8,128)(2,1)} %pad_maximum_fusion.raw_ref, bf16[16,18432]{1,0:T(8,128)(2,1)} %collective-permute-done.2.one_ref, bf16[8,18432]{1,0:T(8,128)(2,1)} %copy-done.6), custom_call_target="tpu_custom_call" | custom-call | tf_op jit(solution)/shard_map/pallas_call | solution.py:99
  64.7 12.0 %collective-permute-start.4 = (bf16[8,18432]{1,0:T(8,128)(2,1)}, bf16[8,18432]{1,0:T(8,128)(2,1)S(1)}, u32[]{:S(2)}, u32[]{:S(2)}) collective-permute-start(bf16[8,18432]{1,0:T(8,128)(2,1)} %get-tuple-element.412), channel_id=1, source_target_pairs={{0,1},{1,0},{2,3},{3,2},{4,5},{5,4},{6,7},{7,6},{8,9},{9,8},{10,11... | collective-permute-start | bytes 884744 | tf_op jit(solution)/shard_map/ppermute | solution.py:30
  76.7 1.4 collective-permute-done.4
  78.1 1.0 add.133.refs_4_
  79.6 6.8 %collective-permute-done.7.refs_5_ = bf16[8,18432]{1,0:T(8,128)(2,1)S(1)} collective-permute-done((bf16[8,18432]{1,0:T(8,128)(2,1)S(1)}, bf16[8,18432]{1,0:T(8,128)(2,1)S(1)}, u32[]{:S(2)}, u32[]{:S(2)}) %collective-permute-start.7) | collective-permute-done | bytes 294944 | tf_op jit(solution)/shard_map/ppermute | solution.py:258
  86.6 0.9 collective-permute-start.8
  87.5 4.3 %collective-permute-done.9.refs_6_ = bf16[8,9216]{1,0:T(8,128)(2,1)S(1)} collective-permute-done((bf16[8,9216]{1,0:T(8,128)(2,1)S(1)}, bf16[8,9216]{1,0:T(8,128)(2,1)S(1)}, u32[]{:S(2)}, u32[]{:S(2)}) %collective-permute-start.9) | collective-permute-done | bytes 147488 | tf_op jit(solution)/shard_map/ppermute | solution.py:266
  91.8 1.6 collective-permute-done.8.refs_7_
  93.4 3.6 %collective-permute-done.10.refs_8_ = bf16[8,9216]{1,0:T(8,128)(2,1)S(1)} collective-permute-done((bf16[8,9216]{1,0:T(8,128)(2,1)S(1)}, bf16[8,9216]{1,0:T(8,128)(2,1)S(1)}, u32[]{:S(2)}, u32[]{:S(2)}) %collective-permute-start.10) | collective-permute-done | bytes 147488 | tf_op jit(solution)/shard_map/ppermute | solution.py:266
  97.0 1.6 collective-permute-done.11.refs_9_
  98.6 3.6 %collective-permute-done.12.refs_10_ = bf16[8,9216]{1,0:T(8,128)(2,1)S(1)} collective-permute-done((bf16[8,9216]{1,0:T(8,128)(2,1)S(1)}, bf16[8,9216]{1,0:T(8,128)(2,1)S(1)}, u32[]{:S(2)}, u32[]{:S(2)}) %collective-permute-start.12) | collective-permute-done | bytes 147488 | tf_op jit(solution)/shard_map/ppermute | solution.py:266
  102.2 1.6 collective-permute-done.13.refs_11_
  103.8 3.6 %collective-permute-done.14.refs_12_ = bf16[8,9216]{1,0:T(8,128)(2,1)S(1)} collective-permute-done((bf16[8,9216]{1,0:T(8,128)(2,1)S(1)}, bf16[8,9216]{1,0:T(8,128)(2,1)S(1)}, u32[]{:S(2)}, u32[]{:S(2)}) %collective-permute-start.14) | collective-permute-done | bytes 147488 | tf_op jit(solution)/shard_map/ppermute | solution.py:266
  107.4 1.6 collective-permute-done.15.refs_13_
  109.0 3.6 %collective-permute-done.16.refs_14_ = bf16[8,9216]{1,0:T(8,128)(2,1)S(1)} collective-permute-done((bf16[8,9216]{1,0:T(8,128)(2,1)S(1)}, bf16[8,9216]{1,0:T(8,128)(2,1)S(1)}, u32[]{:S(2)}, u32[]{:S(2)}) %collective-permute-start.16) | collective-permute-done | bytes 147488 | tf_op jit(solution)/shard_map/ppermute | solution.py:266
  112.6 1.6 collective-permute-done.17.refs_15_
  114.2 3.6 %collective-permute-done.18.refs_16_ = bf16[8,9216]{1,0:T(8,128)(2,1)S(1)} collective-permute-done((bf16[8,9216]{1,0:T(8,128)(2,1)S(1)}, bf16[8,9216]{1,0:T(8,128)(2,1)S(1)}, u32[]{:S(2)}, u32[]{:S(2)}) %collective-permute-start.18) | collective-permute-done | bytes 147488 | tf_op jit(solution)/shard_map/ppermute | solution.py:266
  117.8 1.6 collective-permute-done.19.refs_17_
  119.4 3.6 %collective-permute-done.20.refs_18_ = bf16[8,9216]{1,0:T(8,128)(2,1)S(1)} collective-permute-done((bf16[8,9216]{1,0:T(8,128)(2,1)S(1)}, bf16[8,9216]{1,0:T(8,128)(2,1)S(1)}, u32[]{:S(2)}, u32[]{:S(2)}) %collective-permute-start.20) | collective-permute-done | bytes 147488 | tf_op jit(solution)/shard_map/ppermute | solution.py:266
  123.0 1.6 collective-permute-done.21.refs_19_
  124.6 3.6 %collective-permute-done.22.refs_20_ = bf16[8,9216]{1,0:T(8,128)(2,1)S(1)} collective-permute-done((bf16[8,9216]{1,0:T(8,128)(2,1)S(1)}, bf16[8,9216]{1,0:T(8,128)(2,1)S(1)}, u32[]{:S(2)}, u32[]{:S(2)}) %collective-permute-start.22) | collective-permute-done | bytes 147488 | tf_op jit(solution)/shard_map/ppermute | solution.py:266
  128.2 1.6 collective-permute-done.23.refs_21_
  129.8 3.6 %collective-permute-done.24.refs_22_ = bf16[8,9216]{1,0:T(8,128)(2,1)S(1)} collective-permute-done((bf16[8,9216]{1,0:T(8,128)(2,1)S(1)}, bf16[8,9216]{1,0:T(8,128)(2,1)S(1)}, u32[]{:S(2)}, u32[]{:S(2)}) %collective-permute-start.24) | collective-permute-done | bytes 147488 | tf_op jit(solution)/shard_map/ppermute | solution.py:266
  133.4 1.6 collective-permute-done.25.refs_23_
  135.0 3.6 %collective-permute-done.26.refs_24_ = bf16[8,9216]{1,0:T(8,128)(2,1)S(1)} collective-permute-done((bf16[8,9216]{1,0:T(8,128)(2,1)S(1)}, bf16[8,9216]{1,0:T(8,128)(2,1)S(1)}, u32[]{:S(2)}, u32[]{:S(2)}) %collective-permute-start.26) | collective-permute-done | bytes 147488 | tf_op jit(solution)/shard_map/ppermute | solution.py:266
  138.6 1.6 collective-permute-done.27.refs_25_
  140.2 3.6 %collective-permute-done.28.refs_26_ = bf16[8,9216]{1,0:T(8,128)(2,1)S(1)} collective-permute-done((bf16[8,9216]{1,0:T(8,128)(2,1)S(1)}, bf16[8,9216]{1,0:T(8,128)(2,1)S(1)}, u32[]{:S(2)}, u32[]{:S(2)}) %collective-permute-start.28) | collective-permute-done | bytes 147488 | tf_op jit(solution)/shard_map/ppermute | solution.py:266
  143.8 1.6 collective-permute-done.29.refs_27_
  145.4 3.6 %collective-permute-done.30.refs_28_ = bf16[8,9216]{1,0:T(8,128)(2,1)S(1)} collective-permute-done((bf16[8,9216]{1,0:T(8,128)(2,1)S(1)}, bf16[8,9216]{1,0:T(8,128)(2,1)S(1)}, u32[]{:S(2)}, u32[]{:S(2)}) %collective-permute-start.30) | collective-permute-done | bytes 147488 | tf_op jit(solution)/shard_map/ppermute | solution.py:266
  149.1 1.6 collective-permute-done.31.refs_29_
  150.6 3.6 %collective-permute-done.32.refs_30_ = bf16[8,9216]{1,0:T(8,128)(2,1)S(1)} collective-permute-done((bf16[8,9216]{1,0:T(8,128)(2,1)S(1)}, bf16[8,9216]{1,0:T(8,128)(2,1)S(1)}, u32[]{:S(2)}, u32[]{:S(2)}) %collective-permute-start.32) | collective-permute-done | bytes 147488 | tf_op jit(solution)/shard_map/ppermute | solution.py:266
  154.3 1.6 collective-permute-done.33.refs_31_
  156.2 16.4 %collective-permute-start.6 = (bf16[256,4096]{1,0:T(8,128)(2,1)S(1)}, bf16[256,4096]{1,0:T(8,128)(2,1)S(1)}, u32[]{:S(2)}, u32[]{:S(2)}) collective-permute-start(bf16[256,4096]{1,0:T(8,128)(2,1)S(1)} %copy-done), channel_id=1, source_target_pairs={{0,1},{1,0},{2,3},{3,2},{4,5},{5,4},{6,7},{7,6},{8,9},{9,8},{10,11... | collective-permute-start | bytes 6291464 | tf_op jit(solution)/shard_map/ppermute | solution.py:30
  173.6 1.3 slice.95
  175.6 0.8 collective-permute-done.6.refs_3_
  176.4 1.4 copy-done.1
  177.8 1.8 collective-permute-done.36.refs_34_
  180.3 15.6 %shard_map.67 = f32[8,8]{1,0:T(8,128)S(1)} custom-call(s32[4]{0:T(128)} %pad_add_fusion.1.lens_ref, s32[2]{0:T(128)} %pad_add_fusion.seat_ref, s32[2]{0:T(128)} %get-tuple-element.411.routed_ref, bf16[256,14336]{1,0:T(8,128)(2,1)} %refs_0_.1, bf16[256,14336]{1,0:T(8,128)(2,1)} %collective-permute-done.5.refs_1_, bf16[256,4096]{1,0:T(8,128)(2,1)S(1)} %copy-done, ...), custom_call_target="tpu_custom_call" | custom-call | tf_op jit(solution)/shard_map/pallas_call | solution.py:187
  195.9 3.7 %collective-permute-start.37 = (f32[2,8]{1,0:T(2,128)S(1)}, f32[2,8]{1,0:T(2,128)S(1)}, u32[]{:S(2)}, u32[]{:S(2)}) collective-permute-start(f32[2,8]{1,0:T(2,128)S(1)} %slice.100), channel_id=1, source_target_pairs={{0,1},{1,0},{2,3},{3,2},{4,5},{5,4},{6,7},{7,6},{8,9},{9,8},{10,11... | collective-permute-start | bytes 200 | tf_op jit(solution)/shard_map/ppermute | solution.py:30
  199.6 0.8 collective-permute-done.37
  (133 shorter events, 5.4 us)
Async XLA Ops:
  3.6 22.0 %collective-permute-start.1 = (bf16[24,9344]{1,0:T(8,128)(2,1)S(1)}, bf16[24,9344]{1,0:T(8,128)(2,1)S(1)}, u32[]{:S(2)}, u32[]{:S(2)}) collective-permute-start(bf16[24,9344]{1,0:T(8,128)(2,1)S(1)} %maximum_maximum_fusion), channel_id=1, source_target_pairs={{0,1},{1,0},{2,3},{3,2},{4,5},{5,4},{6,7},{7,6},{8,9},{9,8},{10,11... | collective-permute-start | bytes 1345544 | tf_op jit(solution)/shard_map/ppermute | solution.py:30
  28.7 127.4 %copy-start.34 = (s32[2]{0:T(128)S(1)}, s32[2]{0:T(128)}, u32[]{:S(2)}) copy-start(s32[2]{0:T(128)} %param.12) | copy-start | bytes 28
  28.7 127.5 %copy-start = (bf16[256,4096]{1,0:T(8,128)(2,1)S(1)}, bf16[256,4096]{1,0:T(8,128)(2,1)}, u32[]{:S(2)}) copy-start(bf16[256,4096]{1,0:T(8,128)(2,1)} %refs_2_.1) | copy-start | bytes 6291460
  28.7 31.1 %collective-permute-start.2 = (bf16[16,18432]{1,0:T(8,128)(2,1)S(1)}, bf16[16,18432]{1,0:T(8,128)(2,1)}, u32[]{:S(2)}, u32[]{:S(2)}) collective-permute-start(bf16[16,18432]{1,0:T(8,128)(2,1)S(1)} %convolution_convert_fusion), channel_id=1, source_target_pairs={{1,3},{3,5},{5,7},{7,9},{9,11},{11,13},{13,15},{15,17},{17,19},{19... | collective-permute-start | bytes 1769480 | tf_op jit(solution)/shard_map/ppermute | solution.py:244
  28.9 30.9 %collective-permute-start.3 = (bf16[8,18432]{1,0:T(8,128)(2,1)S(1)}, bf16[8,18432]{1,0:T(8,128)(2,1)S(1)}, u32[]{:S(2)}, u32[]{:S(2)}) collective-permute-start(bf16[8,18432]{1,0:T(8,128)(2,1)S(1)} %slice_select_fusion), channel_id=1, source_target_pairs={{1,5},{3,7},{5,9},{7,11},{9,13},{11,15},{13,17},{15,19},{17,21},{1... | collective-permute-start | bytes 884744 | tf_op jit(solution)/shard_map/ppermute | solution.py:245
  64.7 13.4 %collective-permute-start.4 = (bf16[8,18432]{1,0:T(8,128)(2,1)}, bf16[8,18432]{1,0:T(8,128)(2,1)S(1)}, u32[]{:S(2)}, u32[]{:S(2)}) collective-permute-start(bf16[8,18432]{1,0:T(8,128)(2,1)} %get-tuple-element.412), channel_id=1, source_target_pairs={{0,1},{1,0},{2,3},{3,2},{4,5},{5,4},{6,7},{7,6},{8,9},{9,8},{10,11... | collective-permute-start | bytes 884744 | tf_op jit(solution)/shard_map/ppermute | solution.py:30
  79.1 100.5 %copy-start.2 = (bf16[8,18432]{1,0:T(8,128)(2,1)}, bf16[8,18432]{1,0:T(8,128)(2,1)S(1)}, u32[]{:S(2)}) copy-start(bf16[8,18432]{1,0:T(8,128)(2,1)S(1)} %add.133.refs_4_) | copy-start | bytes 884740
  79.1 100.4 %collective-permute-start.5 = (bf16[256,14336]{1,0:T(8,128)(2,1)}, bf16[256,14336]{1,0:T(8,128)(2,1)}, u32[]{:S(2)}, u32[]{:S(2)}) collective-permute-start(bf16[256,14336]{1,0:T(8,128)(2,1)} %refs_0_.1), channel_id=1, source_target_pairs={{0,1},{1,0},{2,3},{3,2},{4,5},{5,4},{6,7},{7,6},{8,9},{9,8},{10,11... | collective-permute-start | bytes 22020104 | tf_op jit(solution)/shard_map/ppermute | solution.py:30
  79.6 6.8 %collective-permute-start.7 = (bf16[8,18432]{1,0:T(8,128)(2,1)S(1)}, bf16[8,18432]{1,0:T(8,128)(2,1)S(1)}, u32[]{:S(2)}, u32[]{:S(2)}) collective-permute-start(bf16[8,18432]{1,0:T(8,128)(2,1)S(1)} %add.133.refs_4_), channel_id=1, source_target_pairs={{1,3},{3,5},{5,7},{7,9},{9,11},{11,13},{13,15},{15,17},{17,19},{19... | collective-permute-start | bytes 884744 | tf_op jit(solution)/shard_map/ppermute | solution.py:258
  86.4 93.2 %copy-start.3 = (bf16[8,18432]{1,0:T(8,128)(2,1)}, bf16[8,18432]{1,0:T(8,128)(2,1)S(1)}, u32[]{:S(2)}) copy-start(bf16[8,18432]{1,0:T(8,128)(2,1)S(1)} %collective-permute-done.7.refs_5_) | copy-start | bytes 884740
  86.5 5.3 %collective-permute-start.9 = (bf16[8,9216]{1,0:T(8,128)(2,1)S(1)}, bf16[8,9216]{1,0:T(8,128)(2,1)S(1)}, u32[]{:S(2)}, u32[]{:S(2)}) collective-permute-start(bf16[8,9216]{1,0:T(8,128)(2,1)S(1)} %get-tuple-element.585), channel_id=1, source_target_pairs={{1,3},{3,5},{5,7},{7,9},{9,11},{11,13},{13,15},{15,17},{17,19},{19... | collective-permute-start | bytes 442376 | tf_op jit(solution)/shard_map/ppermute | solution.py:266
  86.6 6.8 %collective-permute-start.8 = (bf16[8,9216]{1,0:T(8,128)(2,1)S(1)}, bf16[8,9216]{1,0:T(8,128)(2,1)S(1)}, u32[]{:S(2)}, u32[]{:S(2)}) collective-permute-start(bf16[8,9216]{1,0:T(8,128)(2,1)S(1)} %get-tuple-element.586), channel_id=1, source_target_pairs={{1,3},{3,5},{5,7},{7,9},{9,11},{11,13},{13,15},{15,17},{17,19},{19... | collective-permute-start | bytes 442376 | tf_op jit(solution)/shard_map/ppermute | solution.py:266
  91.8 87.8 %copy-start.8 = (bf16[8,9216]{1,0:T(8,128)(2,1)}, bf16[8,9216]{1,0:T(8,128)(2,1)S(1)}, u32[]{:S(2)}) copy-start(bf16[8,9216]{1,0:T(8,128)(2,1)S(1)} %collective-permute-done.9.refs_6_) | copy-start | bytes 442372
  91.8 5.2 %collective-permute-start.10 = (bf16[8,9216]{1,0:T(8,128)(2,1)S(1)}, bf16[8,9216]{1,0:T(8,128)(2,1)S(1)}, u32[]{:S(2)}, u32[]{:S(2)}) collective-permute-start(bf16[8,9216]{1,0:T(8,128)(2,1)S(1)} %collective-permute-done.9.refs_6_), channel_id=1, source_target_pairs={{1,3},{3,5},{5,7},{7,9},{9,11},{11,13},{13,15},{15,17},{17,19},{19... | collective-permute-start | bytes 442376 | tf_op jit(solution)/shard_map/ppermute | solution.py:266
  93.4 79.3 %copy-start.9 = (bf16[8,9216]{1,0:T(8,128)(2,1)}, bf16[8,9216]{1,0:T(8,128)(2,1)S(1)}, u32[]{:S(2)}) copy-start(bf16[8,9216]{1,0:T(8,128)(2,1)S(1)} %collective-permute-done.8.refs_7_) | copy-start | bytes 442372
  93.4 5.2 %collective-permute-start.11 = (bf16[8,9216]{1,0:T(8,128)(2,1)S(1)}, bf16[8,9216]{1,0:T(8,128)(2,1)S(1)}, u32[]{:S(2)}, u32[]{:S(2)}) collective-permute-start(bf16[8,9216]{1,0:T(8,128)(2,1)S(1)} %collective-permute-done.8.refs_7_), channel_id=1, source_target_pairs={{1,3},{3,5},{5,7},{7,9},{9,11},{11,13},{13,15},{15,17},{17,19},{19... | collective-permute-start | bytes 442376 | tf_op jit(solution)/shard_map/ppermute | solution.py:266
  97.0 57.3 %copy-start.10 = (bf16[8,9216]{1,0:T(8,128)(2,1)}, bf16[8,9216]{1,0:T(8,128)(2,1)S(1)}, u32[]{:S(2)}) copy-start(bf16[8,9216]{1,0:T(8,128)(2,1)S(1)} %collective-permute-done.10.refs_8_) | copy-start | bytes 442372
  97.0 5.2 %collective-permute-start.12 = (bf16[8,9216]{1,0:T(8,128)(2,1)S(1)}, bf16[8,9216]{1,0:T(8,128)(2,1)S(1)}, u32[]{:S(2)}, u32[]{:S(2)}) collective-permute-start(bf16[8,9216]{1,0:T(8,128)(2,1)S(1)} %collective-permute-done.10.refs_8_), channel_id=1, source_target_pairs={{1,3},{3,5},{5,7},{7,9},{9,11},{11,13},{13,15},{15,17},{17,19},{19... | collective-permute-start | bytes 442376 | tf_op jit(solution)/shard_map/ppermute | solution.py:266
  98.6 52.1 %copy-start.11 = (bf16[8,9216]{1,0:T(8,128)(2,1)}, bf16[8,9216]{1,0:T(8,128)(2,1)S(1)}, u32[]{:S(2)}) copy-start(bf16[8,9216]{1,0:T(8,128)(2,1)S(1)} %collective-permute-done.11.refs_9_) | copy-start | bytes 442372
  98.6 5.2 %collective-permute-start.13 = (bf16[8,9216]{1,0:T(8,128)(2,1)S(1)}, bf16[8,9216]{1,0:T(8,128)(2,1)S(1)}, u32[]{:S(2)}, u32[]{:S(2)}) collective-permute-start(bf16[8,9216]{1,0:T(8,128)(2,1)S(1)} %collective-permute-done.11.refs_9_), channel_id=1, source_target_pairs={{1,3},{3,5},{5,7},{7,9},{9,11},{11,13},{13,15},{15,17},{17,19},{19... | collective-permute-start | bytes 442376 | tf_op jit(solution)/shard_map/ppermute | solution.py:266
  102.2 70.5 %copy-start.12 = (bf16[8,9216]{1,0:T(8,128)(2,1)}, bf16[8,9216]{1,0:T(8,128)(2,1)S(1)}, u32[]{:S(2)}) copy-start(bf16[8,9216]{1,0:T(8,128)(2,1)S(1)} %collective-permute-done.12.refs_10_) | copy-start | bytes 442372
  102.2 5.2 %collective-permute-start.14 = (bf16[8,9216]{1,0:T(8,128)(2,1)S(1)}, bf16[8,9216]{1,0:T(8,128)(2,1)S(1)}, u32[]{:S(2)}, u32[]{:S(2)}) collective-permute-start(bf16[8,9216]{1,0:T(8,128)(2,1)S(1)} %collective-permute-done.12.refs_10_), channel_id=1, source_target_pairs={{1,3},{3,5},{5,7},{7,9},{9,11},{11,13},{13,15},{15,17},{17,19},{19... | collective-permute-start | bytes 442376 | tf_op jit(solution)/shard_map/ppermute | solution.py:266
  103.8 52.1 %copy-start.13 = (bf16[8,9216]{1,0:T(8,128)(2,1)}, bf16[8,9216]{1,0:T(8,128)(2,1)S(1)}, u32[]{:S(2)}) copy-start(bf16[8,9216]{1,0:T(8,128)(2,1)S(1)} %collective-permute-done.13.refs_11_) | copy-start | bytes 442372
  103.8 5.2 %collective-permute-start.15 = (bf16[8,9216]{1,0:T(8,128)(2,1)S(1)}, bf16[8,9216]{1,0:T(8,128)(2,1)S(1)}, u32[]{:S(2)}, u32[]{:S(2)}) collective-permute-start(bf16[8,9216]{1,0:T(8,128)(2,1)S(1)} %collective-permute-done.13.refs_11_), channel_id=1, source_target_pairs={{1,3},{3,5},{5,7},{7,9},{9,11},{11,13},{13,15},{15,17},{17,19},{19... | collective-permute-start | bytes 442376 | tf_op jit(solution)/shard_map/ppermute | solution.py:266
  107.4 48.4 %copy-start.14 = (bf16[8,9216]{1,0:T(8,128)(2,1)}, bf16[8,9216]{1,0:T(8,128)(2,1)S(1)}, u32[]{:S(2)}) copy-start(bf16[8,9216]{1,0:T(8,128)(2,1)S(1)} %collective-permute-done.14.refs_12_) | copy-start | bytes 442372
  107.4 5.2 %collective-permute-start.16 = (bf16[8,9216]{1,0:T(8,128)(2,1)S(1)}, bf16[8,9216]{1,0:T(8,128)(2,1)S(1)}, u32[]{:S(2)}, u32[]{:S(2)}) collective-permute-start(bf16[8,9216]{1,0:T(8,128)(2,1)S(1)} %collective-permute-done.14.refs_12_), channel_id=1, source_target_pairs={{1,3},{3,5},{5,7},{7,9},{9,11},{11,13},{13,15},{15,17},{17,19},{19... | collective-permute-start | bytes 442376 | tf_op jit(solution)/shard_map/ppermute | solution.py:266
  109.0 5.2 %collective-permute-start.17 = (bf16[8,9216]{1,0:T(8,128)(2,1)S(1)}, bf16[8,9216]{1,0:T(8,128)(2,1)S(1)}, u32[]{:S(2)}, u32[]{:S(2)}) collective-permute-start(bf16[8,9216]{1,0:T(8,128)(2,1)S(1)} %collective-permute-done.15.refs_13_), channel_id=1, source_target_pairs={{1,3},{3,5},{5,7},{7,9},{9,11},{11,13},{13,15},{15,17},{17,19},{19... | collective-permute-start | bytes 442376 | tf_op jit(solution)/shard_map/ppermute | solution.py:266
  112.6 5.2 %collective-permute-start.18 = (bf16[8,9216]{1,0:T(8,128)(2,1)S(1)}, bf16[8,9216]{1,0:T(8,128)(2,1)S(1)}, u32[]{:S(2)}, u32[]{:S(2)}) collective-permute-start(bf16[8,9216]{1,0:T(8,128)(2,1)S(1)} %collective-permute-done.16.refs_14_), channel_id=1, source_target_pairs={{1,3},{3,5},{5,7},{7,9},{9,11},{11,13},{13,15},{15,17},{17,19},{19... | collective-permute-start | bytes 442376 | tf_op jit(solution)/shard_map/ppermute | solution.py:266
  114.2 5.2 %collective-permute-start.19 = (bf16[8,9216]{1,0:T(8,128)(2,1)S(1)}, bf16[8,9216]{1,0:T(8,128)(2,1)S(1)}, u32[]{:S(2)}, u32[]{:S(2)}) collective-permute-start(bf16[8,9216]{1,0:T(8,128)(2,1)S(1)} %collective-permute-done.17.refs_15_), channel_id=1, source_target_pairs={{1,3},{3,5},{5,7},{7,9},{9,11},{11,13},{13,15},{15,17},{17,19},{19... | collective-permute-start | bytes 442376 | tf_op jit(solution)/shard_map/ppermute | solution.py:266
  117.8 5.2 %collective-permute-start.20 = (bf16[8,9216]{1,0:T(8,128)(2,1)S(1)}, bf16[8,9216]{1,0:T(8,128)(2,1)S(1)}, u32[]{:S(2)}, u32[]{:S(2)}) collective-permute-start(bf16[8,9216]{1,0:T(8,128)(2,1)S(1)} %collective-permute-done.18.refs_16_), channel_id=1, source_target_pairs={{1,3},{3,5},{5,7},{7,9},{9,11},{11,13},{13,15},{15,17},{17,19},{19... | collective-permute-start | bytes 442376 | tf_op jit(solution)/shard_map/ppermute | solution.py:266
  119.4 5.2 %collective-permute-start.21 = (bf16[8,9216]{1,0:T(8,128)(2,1)S(1)}, bf16[8,9216]{1,0:T(8,128)(2,1)S(1)}, u32[]{:S(2)}, u32[]{:S(2)}) collective-permute-start(bf16[8,9216]{1,0:T(8,128)(2,1)S(1)} %collective-permute-done.19.refs_17_), channel_id=1, source_target_pairs={{1,3},{3,5},{5,7},{7,9},{9,11},{11,13},{13,15},{15,17},{17,19},{19... | collective-permute-start | bytes 442376 | tf_op jit(solution)/shard_map/ppermute | solution.py:266
  123.0 5.2 %collective-permute-start.22 = (bf16[8,9216]{1,0:T(8,128)(2,1)S(1)}, bf16[8,9216]{1,0:T(8,128)(2,1)S(1)}, u32[]{:S(2)}, u32[]{:S(2)}) collective-permute-start(bf16[8,9216]{1,0:T(8,128)(2,1)S(1)} %collective-permute-done.20.refs_18_), channel_id=1, source_target_pairs={{1,3},{3,5},{5,7},{7,9},{9,11},{11,13},{13,15},{15,17},{17,19},{19... | collective-permute-start | bytes 442376 | tf_op jit(solution)/shard_map/ppermute | solution.py:266
  124.6 5.2 %collective-permute-start.23 = (bf16[8,9216]{1,0:T(8,128)(2,1)S(1)}, bf16[8,9216]{1,0:T(8,128)(2,1)S(1)}, u32[]{:S(2)}, u32[]{:S(2)}) collective-permute-start(bf16[8,9216]{1,0:T(8,128)(2,1)S(1)} %collective-permute-done.21.refs_19_), channel_id=1, source_target_pairs={{1,3},{3,5},{5,7},{7,9},{9,11},{11,13},{13,15},{15,17},{17,19},{19... | collective-permute-start | bytes 442376 | tf_op jit(solution)/shard_map/ppermute | solution.py:266
  128.2 5.2 %collective-permute-start.24 = (bf16[8,9216]{1,0:T(8,128)(2,1)S(1)}, bf16[8,9216]{1,0:T(8,128)(2,1)S(1)}, u32[]{:S(2)}, u32[]{:S(2)}) collective-permute-start(bf16[8,9216]{1,0:T(8,128)(2,1)S(1)} %collective-permute-done.22.refs_20_), channel_id=1, source_target_pairs={{1,3},{3,5},{5,7},{7,9},{9,11},{11,13},{13,15},{15,17},{17,19},{19... | collective-permute-start | bytes 442376 | tf_op jit(solution)/shard_map/ppermute | solution.py:266
  129.8 5.2 %collective-permute-start.25 = (bf16[8,9216]{1,0:T(8,128)(2,1)S(1)}, bf16[8,9216]{1,0:T(8,128)(2,1)S(1)}, u32[]{:S(2)}, u32[]{:S(2)}) collective-permute-start(bf16[8,9216]{1,0:T(8,128)(2,1)S(1)} %collective-permute-done.23.refs_21_), channel_id=1, source_target_pairs={{1,3},{3,5},{5,7},{7,9},{9,11},{11,13},{13,15},{15,17},{17,19},{19... | collective-permute-start | bytes 442376 | tf_op jit(solution)/shard_map/ppermute | solution.py:266
  133.4 5.2 %collective-permute-start.26 = (bf16[8,9216]{1,0:T(8,128)(2,1)S(1)}, bf16[8,9216]{1,0:T(8,128)(2,1)S(1)}, u32[]{:S(2)}, u32[]{:S(2)}) collective-permute-start(bf16[8,9216]{1,0:T(8,128)(2,1)S(1)} %collective-permute-done.24.refs_22_), channel_id=1, source_target_pairs={{1,3},{3,5},{5,7},{7,9},{9,11},{11,13},{13,15},{15,17},{17,19},{19... | collective-permute-start | bytes 442376 | tf_op jit(solution)/shard_map/ppermute | solution.py:266
  135.0 5.2 %collective-permute-start.27 = (bf16[8,9216]{1,0:T(8,128)(2,1)S(1)}, bf16[8,9216]{1,0:T(8,128)(2,1)S(1)}, u32[]{:S(2)}, u32[]{:S(2)}) collective-permute-start(bf16[8,9216]{1,0:T(8,128)(2,1)S(1)} %collective-permute-done.25.refs_23_), channel_id=1, source_target_pairs={{1,3},{3,5},{5,7},{7,9},{9,11},{11,13},{13,15},{15,17},{17,19},{19... | collective-permute-start | bytes 442376 | tf_op jit(solution)/shard_map/ppermute | solution.py:266
  138.6 5.2 %collective-permute-start.28 = (bf16[8,9216]{1,0:T(8,128)(2,1)S(1)}, bf16[8,9216]{1,0:T(8,128)(2,1)S(1)}, u32[]{:S(2)}, u32[]{:S(2)}) collective-permute-start(bf16[8,9216]{1,0:T(8,128)(2,1)S(1)} %collective-permute-done.26.refs_24_), channel_id=1, source_target_pairs={{1,3},{3,5},{5,7},{7,9},{9,11},{11,13},{13,15},{15,17},{17,19},{19... | collective-permute-start | bytes 442376 | tf_op jit(solution)/shard_map/ppermute | solution.py:266
  140.2 5.2 %collective-permute-start.29 = (bf16[8,9216]{1,0:T(8,128)(2,1)S(1)}, bf16[8,9216]{1,0:T(8,128)(2,1)S(1)}, u32[]{:S(2)}, u32[]{:S(2)}) collective-permute-start(bf16[8,9216]{1,0:T(8,128)(2,1)S(1)} %collective-permute-done.27.refs_25_), channel_id=1, source_target_pairs={{1,3},{3,5},{5,7},{7,9},{9,11},{11,13},{13,15},{15,17},{17,19},{19... | collective-permute-start | bytes 442376 | tf_op jit(solution)/shard_map/ppermute | solution.py:266
  143.8 5.2 %collective-permute-start.30 = (bf16[8,9216]{1,0:T(8,128)(2,1)S(1)}, bf16[8,9216]{1,0:T(8,128)(2,1)S(1)}, u32[]{:S(2)}, u32[]{:S(2)}) collective-permute-start(bf16[8,9216]{1,0:T(8,128)(2,1)S(1)} %collective-permute-done.28.refs_26_), channel_id=1, source_target_pairs={{1,3},{3,5},{5,7},{7,9},{9,11},{11,13},{13,15},{15,17},{17,19},{19... | collective-permute-start | bytes 442376 | tf_op jit(solution)/shard_map/ppermute | solution.py:266
  145.4 5.2 %collective-permute-start.31 = (bf16[8,9216]{1,0:T(8,128)(2,1)S(1)}, bf16[8,9216]{1,0:T(8,128)(2,1)S(1)}, u32[]{:S(2)}, u32[]{:S(2)}) collective-permute-start(bf16[8,9216]{1,0:T(8,128)(2,1)S(1)} %collective-permute-done.29.refs_27_), channel_id=1, source_target_pairs={{1,3},{3,5},{5,7},{7,9},{9,11},{11,13},{13,15},{15,17},{17,19},{19... | collective-permute-start | bytes 442376 | tf_op jit(solution)/shard_map/ppermute | solution.py:266
  149.0 5.2 %collective-permute-start.32 = (bf16[8,9216]{1,0:T(8,128)(2,1)S(1)}, bf16[8,9216]{1,0:T(8,128)(2,1)S(1)}, u32[]{:S(2)}, u32[]{:S(2)}) collective-permute-start(bf16[8,9216]{1,0:T(8,128)(2,1)S(1)} %collective-permute-done.30.refs_28_), channel_id=1, source_target_pairs={{1,3},{3,5},{5,7},{7,9},{9,11},{11,13},{13,15},{15,17},{17,19},{19... | collective-permute-start | bytes 442376 | tf_op jit(solution)/shard_map/ppermute | solution.py:266
  150.6 5.2 %collective-permute-start.33 = (bf16[8,9216]{1,0:T(8,128)(2,1)S(1)}, bf16[8,9216]{1,0:T(8,128)(2,1)S(1)}, u32[]{:S(2)}, u32[]{:S(2)}) collective-permute-start(bf16[8,9216]{1,0:T(8,128)(2,1)S(1)} %collective-permute-done.31.refs_29_), channel_id=1, source_target_pairs={{1,3},{3,5},{5,7},{7,9},{9,11},{11,13},{13,15},{15,17},{17,19},{19... | collective-permute-start | bytes 442376 | tf_op jit(solution)/shard_map/ppermute | solution.py:266
  154.3 18.4 %collective-permute-start.34 = (bf16[8,9216]{1,0:T(8,128)(2,1)S(1)}, bf16[8,9216]{1,0:T(8,128)(2,1)S(1)}, u32[]{:S(2)}, u32[]{:S(2)}) collective-permute-start(bf16[8,9216]{1,0:T(8,128)(2,1)S(1)} %collective-permute-done.32.refs_30_), channel_id=1, source_target_pairs={{1,3},{3,5},{5,7},{7,9},{9,11},{11,13},{13,15},{15,17},{17,19},{19... | collective-permute-start | bytes 442376 | tf_op jit(solution)/shard_map/ppermute | solution.py:266
  156.0 16.6 %collective-permute-start.35 = (bf16[8,9216]{1,0:T(8,128)(2,1)S(1)}, bf16[8,9216]{1,0:T(8,128)(2,1)S(1)}, u32[]{:S(2)}, u32[]{:S(2)}) collective-permute-start(bf16[8,9216]{1,0:T(8,128)(2,1)S(1)} %collective-permute-done.33.refs_31_), channel_id=1, source_target_pairs={{1,3},{3,5},{5,7},{7,9},{9,11},{11,13},{13,15},{15,17},{17,19},{19... | collective-permute-start | bytes 442376 | tf_op jit(solution)/shard_map/ppermute | solution.py:266
  156.2 20.1 %collective-permute-start.6 = (bf16[256,4096]{1,0:T(8,128)(2,1)S(1)}, bf16[256,4096]{1,0:T(8,128)(2,1)S(1)}, u32[]{:S(2)}, u32[]{:S(2)}) collective-permute-start(bf16[256,4096]{1,0:T(8,128)(2,1)S(1)} %copy-done), channel_id=1, source_target_pairs={{0,1},{1,0},{2,3},{3,2},{4,5},{5,4},{6,7},{7,6},{8,9},{9,8},{10,11... | collective-permute-start | bytes 6291464 | tf_op jit(solution)/shard_map/ppermute | solution.py:30
  172.7 6.9 %collective-permute-start.36 = (bf16[8,18432]{1,0:T(8,128)(2,1)S(1)}, bf16[8,18432]{1,0:T(8,128)(2,1)S(1)}, u32[]{:S(2)}, u32[]{:S(2)}) collective-permute-start(bf16[8,18432]{1,0:T(8,128)(2,1)S(1)} %pad_maximum_fusion.2), channel_id=1, source_target_pairs={{1,3},{3,5},{5,7},{7,9},{9,11},{11,13},{13,15},{15,17},{17,19},{19... | collective-permute-start | bytes 884744 | tf_op jit(solution)/shard_map/ppermute | solution.py:267
  195.9 4.5 %collective-permute-start.37 = (f32[2,8]{1,0:T(2,128)S(1)}, f32[2,8]{1,0:T(2,128)S(1)}, u32[]{:S(2)}, u32[]{:S(2)}) collective-permute-start(f32[2,8]{1,0:T(2,128)S(1)} %slice.100), channel_id=1, source_target_pairs={{0,1},{1,0},{2,3},{3,2},{4,5},{5,4},{6,7},{7,6},{8,9},{9,8},{10,11... | collective-permute-start | bytes 200 | tf_op jit(solution)/shard_map/ppermute | solution.py:30
  (26 other events, 491.6 us)
